TPU v7x, 32 devices: a whole 2x2x4 slice. The times are simulated.
32 devices in a mesh: span: 4 (over y, x), model: 8 (over z, core).
Axes of the slice: x: 2, y: 2, z: 4, core: 2. Of those that a mesh axis runs over, the one named last changes fastest.
Arguments:
- latents: bfloat16 [4, 2048, 512], P(None, ('span', 'model')), may hold values from -6 to 6
- rotary_rows: bfloat16 [4, 2048, 64], P(None, ('span', 'model')), may hold values from -6 to 6
- latent_gain: float32 [512], replicated, may hold values from 0.25 to 1.75
- key_up: bfloat16 [512, 16, 128], P(None, 'model'), may hold values from -0.25 to 0.25
- value_up: bfloat16 [512, 16, 128], P(None, 'model'), may hold values from -0.25 to 0.25
Outputs:
- decode_keys: bfloat16 [4, 16, 192, 2048], P('span', 'model')
- decode_values: bfloat16 [4, 2048, 16, 128], P('span', None, 'model')
All inputs are finite; a program needn't handle non-finite values.
Results may differ from a plain program's by a relative error of at most 0.0049.
Values may be sent and summed in bfloat16 or wider, within the bound.
No kernel may reach another device: no remote copies, remote signals or barrier semaphores. Data moves between devices by JAX's collectives and lax.ppermute only.
A program may use at most 64 MiB of HBM per device.

v0:
```python
import jax
import jax.numpy as jnp
from jax import lax
from jax.sharding import PartitionSpec as P


def widen_rows(rows, rotary, key_up, value_up):
    wide_keys = jnp.einsum(
        "btr,rhk->bthk", rows, key_up, preferred_element_type=jnp.float32
    ).astype(jnp.bfloat16)
    shared = jnp.broadcast_to(rotary[:, :, None], wide_keys.shape[:3] + rotary.shape[2:])
    wide_values = jnp.einsum(
        "btr,rhk->bthk", rows, value_up, preferred_element_type=jnp.float32
    ).astype(jnp.bfloat16)
    return (jnp.concatenate([wide_keys, shared], axis=-1), wide_values)


def scale_rows(vectors, row_gain):
    return (
        vectors * lax.rsqrt(jnp.mean(vectors * vectors, axis=-1, keepdims=True) + 1e-06) * row_gain
    )


def shards(latents, rotary_rows, latent_gain, key_up, value_up):
    rows_ready = scale_rows(latents.astype(jnp.float32), latent_gain).astype(jnp.bfloat16)
    rows_moved, rotary_moved = (
        lax.all_to_all(rows_ready, "span", split_axis=0, concat_axis=1, tiled=True),
        lax.all_to_all(rotary_rows, "span", split_axis=0, concat_axis=1, tiled=True),
    )
    rows_cut = rows_moved.reshape(
        rows_moved.shape[0], lax.axis_size("span"), -1, rows_moved.shape[2]
    )
    rotary_cut = rotary_moved.reshape(
        rotary_moved.shape[0], lax.axis_size("span"), -1, rotary_moved.shape[2]
    )
    rows_joined, rotary_joined = (
        lax.all_gather(rows_cut, "model", axis=2, tiled=True),
        lax.all_gather(rotary_cut, "model", axis=2, tiled=True),
    )
    rows_whole = rows_joined.reshape(rows_joined.shape[0], -1, rows_joined.shape[3])
    rotary_whole = rotary_joined.reshape(rotary_joined.shape[0], -1, rotary_joined.shape[3])
    decode_keys, decode_values = widen_rows(rows_whole, rotary_whole, key_up, value_up)
    decode_keys = jnp.transpose(decode_keys, (0, 2, 3, 1))
    return (decode_keys, decode_values)


def solution(mesh):
    placed = (
        P(None, ("span", "model"), None),
        P(None, ("span", "model"), None),
        P(),
        P(None, "model", None),
        P(None, "model", None),
    )
    return jax.shard_map(
        shards,
        mesh=mesh,
        in_specs=placed,
        out_specs=(P("span", "model", None, None), P("span", None, "model", None)),
        check_vma=False,
    )
```

profile of v0, /device:TPU:0, one launch (start us, length us, event | category | flops | bytes accessed | tf_op | source)
XLA Modules:
  0.0 75.8 jit_solution(13271837886487071858)
XLA Ops:
  7.2 0.0 copy-start
  7.2 0.0 all-gather.4.cloned.1.call-start
  7.2 1.1 %fusion.1 = f32[4,64]{1,0:T(4,128)S(1)} fusion(bf16[4,64,512]{2,1,0:T(8,128)(2,1)} %param.5), kind=kLoop, calls=%fused_computation.6 | loop fusion | flops 392960 | bytes 263168 | tf_op jit(solution)/shard_map/reduce_sum | solution.py:20
  8.4 1.1 %fusion.3 = bf16[4,64,512]{2,1,0:T(8,128)(2,1)S(1)} fusion(bf16[4,64,512]{2,1,0:T(8,128)(2,1)} %param.5, f32[512]{0:T(512)} %param.7, f32[4,64]{1,0:T(4,128)S(1)} %add_rsqrt_fusion), kind=kLoop, calls=%fused_computation.8 | loop fusion | flops 524288 | bytes 527360 | tf_op jit(solution)/shard_map/convert_element_type | solution.py:25
  9.4 10.8 %all_to_all.8 = bf16[4,64,512]{2,1,0:T(8,128)(2,1)} all-to-all(bf16[4,64,512]{2,1,0:T(8,128)(2,1)S(1)} %fusion.3), channel_id=1, replica_groups=mesh['span'=4,'model'=8] {'span'}, dimensions={0} | all-to-all | bytes 524288 | tf_op jit(solution)/shard_map/all_to_all | solution.py:27
  20.3 0.0 all-gather.4.cloned.1.call-update
  20.3 1.6 %reshape.51 = bf16[4,2,2048]{2,1,0:T(2,128)(2,1)} reshape(bf16[4,64,64]{2,1,0:T(8,128)(2,1)} %param.6) | data formatting | bytes 65536
  21.9 3.3 %all-to-all-start.1 = ((bf16[4,2,2048]{2,1,0:T(2,128)(2,1)}), bf16[4,2,2048]{2,1,0:T(2,128)(2,1)S(1)}, u32[]{:S(2)}, u32[]{:S(2)}) async-start(bf16[4,2,2048]{2,1,0:T(2,128)(2,1)} %reshape.51), calls=%async_computation.1 | async-start | bytes 65536 | tf_op jit(solution)/shard_map/all_to_all | solution.py:28
  25.1 1.1 %copy.7 = bf16[512,2,128]{0,2,1:T(8,128)(2,1)S(1)} copy(bf16[512,2,128]{2,1,0:T(2,128)(2,1)} %param.8) | data formatting | bytes 524288 | tf_op args[3]
  26.3 3.6 %all-to-all-done.1 = bf16[4,2,2048]{2,1,0:T(2,128)(2,1)S(1)} async-done(((bf16[4,2,2048]{2,1,0:T(2,128)(2,1)}), bf16[4,2,2048]{2,1,0:T(2,128)(2,1)S(1)}, u32[]{:S(2)}, u32[]{:S(2)}) %all-to-all-start.1) | async-done | bytes 32800 | tf_op jit(solution)/shard_map/all_to_all | solution.py:28
  29.9 0.1 reshape.52
  30.0 17.8 %all-gather.1 = bf16[4,512,64]{2,1,0:T(8,128)(2,1)S(1)} all-gather(bf16[4,64,64]{2,1,0:T(8,128)(2,1)S(1)} %reshape.52), channel_id=3, replica_groups=mesh['span'=4,'model'=8] {'model'}, dimensions={1}, use_global_device_ids=true | all-gather | bytes 294912 | tf_op jit(solution)/shard_map/all_gather | solution.py:38
  47.8 0.2 copy.8
  48.0 5.5 %all-gather.4.cloned.1.call-done = bf16[4,512,512]{2,1,0:T(8,128)(2,1)} async-done(((bf16[4,64,512]{2,1,0:T(8,128)(2,1)}), bf16[4,512,512]{2,1,0:T(8,128)(2,1)}) %all-gather.4.cloned.1.call-update) | async-done | bytes 2097168 | tf_op jit(solution)/shard_map/all_gather | solution.py:37
  53.5 2.3 %fusion.5 = f32[2048,256]{0,1:S(1)} fusion(bf16[2048,512]{1,0:T(8,128)(2,1)} %bitcast.16, bf16[512,256]{0,1:T(8,128)(2,1)S(1)} %bitcast.19), kind=kOutput, calls=%fused_computation.11 | convolution fusion | flops 536870912 | bytes 4456448
  55.9 0.0 copy-start.1
  55.9 0.1 convert_bitcast_fusion
  56.0 0.0 copy-done
  56.0 1.4 %copy-done.1 = bf16[4,512,512]{2,1,0:T(8,128)(2,1)S(1)} copy-done((bf16[4,512,512]{2,1,0:T(8,128)(2,1)S(1)}, bf16[4,512,512]{2,1,0:T(8,128)(2,1)}, u32[]{:S(2)}) %copy-start.1) | copy-done | bytes 2097176
  57.5 0.7 fusion
  58.2 9.5 %copy.10 = bf16[1,2048,2,128]{3,2,1,0:T(2,128)(2,1)} copy(bf16[1,2048,2,128]{3,1,2,0:T(8,128)(2,1)S(1)} %fusion) | data formatting | bytes 2097152
  67.7 1.2 %maximum_bitcast_fusion = bf16[1,2,192,2048]{3,2,1,0:T(8,128)(2,1)} fusion(bf16[1,2048,2,64]{1,3,2,0:T(8,128)(2,1)S(1)} %broadcast_in_dim.10, bf16[1,2048,2,128]{1,3,2,0:T(8,128)(2,1)S(1)} %convert_bitcast_fusion), kind=kLoop, calls=%fused_computation.2 | loop fusion | flops 3145728 | bytes 3145728 | tf_op jit(solution)/shard_map/transpose | solution.py:43
  (2 shorter events, 0.0 us)
Async XLA Ops:
  7.2 48.9 %copy-start = (bf16[512,2,128]{2,1,0:T(2,128)(2,1)S(1)}, bf16[512,2,128]{2,1,0:T(2,128)(2,1)}, u32[]{:S(2)}) copy-start(bf16[512,2,128]{2,1,0:T(2,128)(2,1)} %param.9) | copy-start | bytes 786436
  7.2 46.3 %all-gather.4.cloned.1.call-start = ((), (), s32[]{:S(2)}) async-start(), calls=%async_computation.2 | async-start | bytes 2359296 | tf_op jit(solution)/shard_map/all_gather | solution.py:37
  21.9 8.0 %all-to-all-start.1 = ((bf16[4,2,2048]{2,1,0:T(2,128)(2,1)}), bf16[4,2,2048]{2,1,0:T(2,128)(2,1)S(1)}, u32[]{:S(2)}, u32[]{:S(2)}) async-start(bf16[4,2,2048]{2,1,0:T(2,128)(2,1)} %reshape.51), calls=%async_computation.1 | async-start | bytes 65536 | tf_op jit(solution)/shard_map/all_to_all | solution.py:28
  55.9 1.6 %copy-start.1 = (bf16[4,512,512]{2,1,0:T(8,128)(2,1)S(1)}, bf16[4,512,512]{2,1,0:T(8,128)(2,1)}, u32[]{:S(2)}) copy-start(bf16[4,512,512]{2,1,0:T(8,128)(2,1)} %all-gather.4.cloned.1.call-done) | copy-start | bytes 6291460
Sparse Core Ops, SparseCore 0:
  20.4 33.0 all-gather.3
where the time goes:
time: 76.2 us; the launch traced here: 75.8 us
  blocking collectives  28.6 us (38%)
  between operations  14.1 us (19%)
  local copies, waits for them, and re-layouts  13.9 us (18%)
  waiting for transfers between devices  9.15 us (12%)
  other arithmetic  3.59 us (5%)
  starting transfers between devices  3.3 us (4%)
  matrix products  3.03 us (4%)
    all_gather x1, blocking collectives, shards(): lax.all_gather(rotary_cut, 'model', axis=2, tiled=True)  17.8 us
    unnamed x8, local copies, waits for them, and re-layouts  13.7 us
    all_to_all x1, blocking collectives, shards(): lax.all_to_all(rows_ready, 'span', split_axis=0, concat_axis=1, tiled=True)  10.8 us
    all_gather x1, waiting for transfers between devices, shards(): lax.all_gather(rows_cut, 'model', axis=2, tiled=True)  5.53 us
    all_to_all x1, waiting for transfers between devices, shards(): lax.all_to_all(rotary_rows, 'span', split_axis=0, concat_axis=1, tiled=True)  3.6 us
    all_to_all x1, starting transfers between devices, shards(): lax.all_to_all(rotary_rows, 'span', split_axis=0, concat_axis=1, tiled=True)  3.26 us
    unnamed x1, matrix products  2.33 us
  transfers between devices with their start and end apart: 2, of which 2 were waited for; matrix products, arithmetic and copies ran while one was open for 4% of the time, Pallas kernels for 0%

commit v1 on v0

v1 whole, which is shorter than its diff:
```python
import jax
import jax.numpy as jnp
from jax import lax
from jax.experimental import pallas as pl
from jax.experimental.pallas import tpu as pltpu
from jax.sharding import PartitionSpec as P

LANES = 128
CHUNKS = 2


def pack_rows(latents, rotary, latent_gain):
    seqs, count, width = latents.shape
    rot = rotary.shape[2]
    fold = LANES // rot
    pieces = width // LANES
    high = pieces * count + count // fold

    def body(rows_ref, rotary_ref, gain_ref, out_ref):
        for s in range(seqs):
            rows = rows_ref[s].astype(jnp.float32)
            scale = lax.rsqrt(jnp.mean(rows * rows, axis=-1, keepdims=True) + 1e-06)
            ready = (rows * scale * gain_ref[...]).astype(jnp.bfloat16)
            for i in range(pieces):
                out_ref[s, i * count : (i + 1) * count] = ready[:, i * LANES : (i + 1) * LANES]
            part = rotary_ref[s].astype(jnp.float32)
            cut = count // fold
            wide = jnp.concatenate([part[i * cut : (i + 1) * cut] for i in range(fold)], axis=1)
            out_ref[s, pieces * count :] = wide.astype(jnp.bfloat16)

    return pl.pallas_call(
        body,
        out_shape=jax.ShapeDtypeStruct((seqs, high, LANES), jnp.bfloat16),
        name="pack",
    )(latents, rotary, latent_gain.reshape(1, -1))


def expand(order, chunks, keys_t, values, count, rot, width, spans, core):
    heads = values.shape[1]
    key_part = keys_t.shape[0] // heads
    value_size = values.shape[2]
    values = values.reshape(width, heads * value_size)
    zs, _, high, _ = chunks[0][0].shape
    cores = len(chunks[0])
    tile = zs * cores * count
    pieces, fold = width // LANES, LANES // rot
    cut = count // fold
    starts = [0]
    for chunk in chunks:
        starts.append(starts[-1] + chunk[0].shape[1])
    refs_of = len(chunks) * cores

    def body(order_ref, *refs):
        ins, (key_ref, value_ref, keys_out, values_out, rows_s, rot_s, wide_s) = (
            refs[:refs_of],
            refs[refs_of:],
        )
        step = pl.program_id(0)
        first = order_ref[spans] == 0

        for j in range(len(chunks)):

            @pl.when((step >= starts[j]) & (step < starts[j + 1]))
            def _(j=j):
                pair = ins[j * cores : (j + 1) * cores]
                for z in range(zs):
                    got = [ref[z, 0] for ref in pair]
                    if cores == 2:
                        got = [
                            jnp.where(first, got[0], got[1]),
                            jnp.where(first, got[1], got[0]),
                        ]
                    for c in range(cores):
                        at = (z * cores + c) * count
                        for i in range(pieces):
                            rows_s[at : at + count, i * LANES : (i + 1) * LANES] = got[c][
                                i * count : (i + 1) * count
                            ]
                        tail = got[c][pieces * count :].astype(jnp.float32)
                        for i in range(fold):
                            rot_s[at + i * cut : at + (i + 1) * cut] = tail[
                                :, i * rot : (i + 1) * rot
                            ].astype(jnp.bfloat16)

        rows = rows_s[...]
        dims = (((1,), (1,)), ((), ()))
        wide_keys = lax.dot_general(key_ref[...], rows, dims, preferred_element_type=jnp.float32)
        wide_keys = wide_keys.astype(jnp.bfloat16)
        eye = (
            lax.broadcasted_iota(jnp.int32, (rot, rot), 0)
            == lax.broadcasted_iota(jnp.int32, (rot, rot), 1)
        ).astype(jnp.float32).astype(jnp.bfloat16)
        shared = lax.dot_general(eye, rot_s[...], dims, preferred_element_type=jnp.float32)
        shared = shared.astype(jnp.bfloat16)
        for h in range(heads):
            keys_out[0, h, :key_part] = wide_keys[h * key_part : (h + 1) * key_part]
            keys_out[0, h, key_part:] = shared
        wide_values = jnp.dot(rows, value_ref[...], preferred_element_type=jnp.float32)
        if heads == 1:
            values_out[...] = wide_values.astype(jnp.bfloat16)
        else:
            for h in range(heads):
                wide_s[pl.ds(h, tile, stride=heads)] = wide_values[
                    :, h * value_size : (h + 1) * value_size
                ]
            values_out[...] = wide_s[...].astype(jnp.bfloat16)

    length = spans * tile
    specs = []
    for j, chunk in enumerate(chunks):
        most = chunk[0].shape[1] - 1
        for _ in chunk:
            specs.append(
                pl.BlockSpec(
                    (zs, 1, high, LANES),
                    lambda i, o, a=starts[j], m=most: (0, jnp.clip(i - a, 0, m), 0, 0),
                )
            )
    whole = lambda i, o: (0, 0)
    decode_keys, decode_values = pl.pallas_call(
        body,
        grid_spec=pltpu.PrefetchScalarGridSpec(
            num_scalar_prefetch=1,
            grid=(spans,),
            in_specs=specs
            + [pl.BlockSpec(keys_t.shape, whole), pl.BlockSpec(values.shape, whole)],
            out_specs=[
                pl.BlockSpec((1, heads, key_part + rot, tile), lambda i, o: (0, 0, 0, o[i])),
                pl.BlockSpec((tile * heads, value_size), lambda i, o: (o[i], 0)),
            ],
            scratch_shapes=[
                pltpu.VMEM((tile, width), jnp.bfloat16),
                pltpu.VMEM((tile, rot), jnp.bfloat16),
                pltpu.VMEM((tile * heads, value_size), jnp.float32),
            ],
        ),
        out_shape=[
            jax.ShapeDtypeStruct((1, heads, key_part + rot, length), jnp.bfloat16),
            jax.ShapeDtypeStruct((length * heads, value_size), jnp.bfloat16),
        ],
        name="expand",
    )(order, *[a for chunk in chunks for a in chunk], keys_t, values)
    return decode_keys, decode_values.reshape(1, length, heads, value_size)


def shards(latents, rotary_rows, latent_gain, key_up, value_up):
    spans, models = lax.axis_size("span"), lax.axis_size("model")
    me, place = lax.axis_index("span"), lax.axis_index("model")
    _, count, width = latents.shape
    rot = rotary_rows.shape[2]
    cores = 2
    core = place % cores
    packed = pack_rows(latents, rotary_rows, latent_gain)
    keys_t = key_up.transpose(1, 2, 0).reshape(-1, width)

    parts = [lax.dynamic_slice_in_dim(packed, me, 1, 0)]
    for k in range(1, spans):
        sent = lax.dynamic_slice_in_dim(packed, me ^ k, 1, 0)
        parts.append(lax.ppermute(sent, "span", [(i, i ^ k) for i in range(spans)]))
    order = jnp.concatenate(
        [me ^ jnp.arange(spans, dtype=jnp.int32), core.astype(jnp.int32)[None]]
    )

    along = [[z * cores + c for z in range(models // cores)] for c in range(cores)]
    swap = [(i, i ^ 1) for i in range(models)]
    chunks, size = [], spans // CHUNKS
    token = None
    for j in range(CHUNKS):
        mine = jnp.concatenate(parts[j * size : (j + 1) * size], axis=0)
        if token is not None:
            mine, _ = lax.optimization_barrier((mine, token))
        own = lax.all_gather(mine, "model", axis_index_groups=along)
        token = own
        chunks.append((own, lax.ppermute(own, "model", swap)))
    return expand(order, chunks, keys_t, value_up, count, rot, width, spans, core)


def solution(mesh):
    placed = (
        P(None, ("span", "model"), None),
        P(None, ("span", "model"), None),
        P(),
        P(None, "model", None),
        P(None, "model", None),
    )
    return jax.shard_map(
        shards,
        mesh=mesh,
        in_specs=placed,
        out_specs=(P("span", "model", None, None), P("span", None, "model", None)),
        check_vma=False,
    )
```

time: 76.2 us -> 52.1 us (0.68)
  between operations: 14.1 us -> 0.69 us
  local copies, waits for them, and re-layouts: 13.9 us -> 3.64 us
  Pallas kernels: 0 us -> 8.17 us
  waiting for transfers between devices: 9.15 us -> 1.05 us
  blocking collectives: 28.6 us -> 32.5 us
  matrix products: 3.03 us -> 0 us
  other arithmetic: 3.59 us -> 0.7 us
  starting transfers between devices: 3.3 us -> 5.08 us
    all_gather x1 -> x2, blocking collectives: 17.8 us -> 32.5 us  [shards(): own = lax.all_gather(mine, 'model', axis_index_groups=along)]
    unnamed x8 -> x13, local copies, waits for them, and re-layouts: 13.7 us -> 1.72 us
    all_to_all x1 -> x0, blocking collectives: 10.8 us -> none  [shards(): lax.all_to_all(rows_ready, 'span', split_axis=0, concat_axis=1, tiled=True)]
    pallas_call x0 -> x2, Pallas kernels: none -> 8.17 us  [the longest x1 6.23 us: expand(): pl.pallas_call(body, grid_spec=pltpu.PrefetchScalarGridSpec(num_scalar_pr...]
    all_gather x1 -> x0, waiting for transfers between devices: 5.53 us -> none  [shards(): lax.all_gather(rows_cut, 'model', axis=2, tiled=True)]
    ppermute x0 -> x5, starting transfers between devices: none -> 5.08 us  [the longest x3 4.57 us: shards(): parts.append(lax.ppermute(sent, 'span', [(i, i ^ k) for i in range(spans)]))]
    all_to_all x1 -> x0, waiting for transfers between devices: 3.6 us -> none  [shards(): lax.all_to_all(rotary_rows, 'span', split_axis=0, concat_axis=1, tiled=True)]
    all_to_all x1 -> x0, starting transfers between devices: 3.26 us -> none  [shards(): lax.all_to_all(rotary_rows, 'span', split_axis=0, concat_axis=1, tiled=True)]
  transfers between devices with their start and end apart: 2 -> 5, of which waited for: 2 -> 2; matrix products, arithmetic and copies ran while one was open for 4% -> 4% of each run, Pallas kernels for 0% -> 0%
where the time goes in v1:
time: 52.1 us; the launch traced here: 51.9 us
  blocking collectives  32.5 us (62%)
  Pallas kernels  8.17 us (16%)
  starting transfers between devices  5.08 us (10%)
  local copies, waits for them, and re-layouts  3.64 us (7%)
  waiting for transfers between devices  1.05 us (2%)
  other arithmetic  0.7 us (1%)
  between operations  0.69 us (1%)
    all_gather x2, blocking collectives, shards(): own = lax.all_gather(mine, 'model', axis_index_groups=along)  32.5 us
    pallas_call x1, Pallas kernels, expand(): pl.pallas_call(body, grid_spec=pltpu.PrefetchScalarGridSpec(num_scalar_pr...  6.23 us
    ppermute x3, starting transfers between devices, shards(): parts.append(lax.ppermute(sent, 'span', [(i, i ^ k) for i in range(spans)]))  4.57 us
    pallas_call x1, Pallas kernels, pack_rows(): pl.pallas_call(body, out_shape=jax.ShapeDtypeStruct((seqs, high, LANES),...  1.93 us
    unnamed x13, local copies, waits for them, and re-layouts  1.72 us
    dynamic_slice x1, local copies, waits for them, and re-layouts, shards(): sent = lax.dynamic_slice_in_dim(packed, me ^ k, 1, 0)  1.05 us
  transfers between devices with their start and end apart: 5, of which 2 were waited for; matrix products, arithmetic and copies ran while one was open for 4% of the time, Pallas kernels for 0%

profile of v1, /device:TPU:0, one launch (start us, length us, event | category | flops | bytes accessed | tf_op | source)
XLA Modules:
  0.0 51.9 jit_solution(15454154181585391299)
XLA Ops:
  0.7 0.0 copy-start.4
  0.7 1.9 %pack.1 = bf16[4,288,128]{2,1,0:T(8,128)(2,1)} custom-call(bf16[4,64,512]{2,1,0:T(8,128)(2,1)} %rows_ref.1, bf16[4,64,64]{2,1,0:T(8,128)(2,1)} %rotary_ref.1, f32[1,512]{1,0:T(1,128)} %bitcast.19), custom_call_target="tpu_custom_call" | custom-call | tf_op jit(solution)/shard_map/pack/pallas_call | solution.py:31
  2.6 0.0 copy-start.5
  2.6 1.1 %constant_dynamic-slice_fusion.1 = (bf16[1,288,128]{2,1,0:T(8,128)(2,1)S(1)}, bf16[1,288,128]{2,1,0:T(8,128)(2,1)S(1)}, bf16[1,288,128]{2,1,0:T(8,128)(2,1)S(1)}, bf16[1,288,128]{2,1,0:T(8,128)(2,1)S(1)}) fusion(bf16[4,288,128]{2,1,0:T(8,128)(2,1)} %pack.1, s32[]{:T(128)S(6)} %select_n.22, s32[]{:T(128)S(6)} %select_n.23, s32[]{:T(128)S(6)} %select_n.21, ...), kind=kLoop, calls=%fused_computation.4 | loop fusion | bytes 589840 | tf_op jit(solution)/shard_map/dynamic_slice | solution.py:158
  3.7 3.0 %collective-permute-start = (bf16[1,288,128]{2,1,0:T(8,128)(2,1)S(1)}, bf16[1,288,128]{2,1,0:T(8,128)(2,1)S(1)}, u32[]{:S(2)}, u32[]{:S(2)}) collective-permute-start(bf16[1,288,128]{2,1,0:T(8,128)(2,1)S(1)} %get-tuple-element.10), channel_id=1, source_target_pairs={{0,8},{8,0},{16,24},{24,16},{1,9},{9,1},{17,25},{25,17},{2,10},{10... | collective-permute-start | bytes 221192 | tf_op jit(solution)/shard_map/ppermute | solution.py:159
  6.7 1.5 %collective-permute-start.2 = (bf16[1,288,128]{2,1,0:T(8,128)(2,1)S(1)}, bf16[1,288,128]{2,1,0:T(8,128)(2,1)S(1)}, u32[]{:S(2)}, u32[]{:S(2)}) collective-permute-start(bf16[1,288,128]{2,1,0:T(8,128)(2,1)S(1)} %get-tuple-element.8), channel_id=1, source_target_pairs={{0,16},{8,24},{16,0},{24,8},{1,17},{9,25},{17,1},{25,9},{2,18},{10... | collective-permute-start | bytes 221192 | tf_op jit(solution)/shard_map/ppermute | solution.py:159
  8.2 0.0 collective-permute-start.3
  8.2 1.0 %collective-permute-done = bf16[1,288,128]{2,1,0:T(8,128)(2,1)S(1)} collective-permute-done((bf16[1,288,128]{2,1,0:T(8,128)(2,1)S(1)}, bf16[1,288,128]{2,1,0:T(8,128)(2,1)S(1)}, u32[]{:S(2)}, u32[]{:S(2)}) %collective-permute-start) | collective-permute-done | bytes 73760 | tf_op jit(solution)/shard_map/ppermute | solution.py:159
  9.2 16.3 %all-gather = bf16[8,288,128]{2,1,0:T(8,128)(2,1)S(1)} all-gather(bf16[2,288,128]{2,1,0:T(8,128)(2,1)S(1)} %pad_maximum_fusion), channel_id=2, replica_groups={{0,2,4,6},{1,3,5,7},{8,10,12,14},{9,11,13,15},{16,18,20,22},{17,19,21,2..., dimensions={0}, use_global_device_ids=true | all-gather | bytes 737280 | tf_op jit(solution)/shard_map/all_gather | solution.py:172
  25.5 0.0 copy-start
  25.5 0.0 collective-permute-done.2
  25.5 0.0 collective-permute-done.3
  25.5 16.3 %all-gather.1 = bf16[8,288,128]{2,1,0:T(8,128)(2,1)S(1)} all-gather(bf16[2,288,128]{2,1,0:T(8,128)(2,1)S(1)} %pad_maximum_fusion.1), channel_id=3, replica_groups={{0,2,4,6},{1,3,5,7},{8,10,12,14},{9,11,13,15},{16,18,20,22},{17,19,21,2..., dimensions={0}, use_global_device_ids=true | all-gather | bytes 737280 | tf_op jit(solution)/shard_map/all_gather | solution.py:172
  41.8 0.0 copy-start.1
  41.8 0.0 collective-permute-start.4
  41.8 0.5 collective-permute-start.1
  42.3 0.0 copy-done.4
  42.3 0.9 %copy.8 = bf16[2,128,512]{2,1,0:T(8,128)(2,1)} copy(bf16[2,128,512]{1,0,2:T(2,128)(2,1)S(1)} %bitcast.17) | data formatting | bytes 524288 | tf_op jit(solution)/shard_map/transpose | solution.py:154
  43.2 0.0 copy-done.5
  43.2 0.7 %copy.11 = bf16[64,8,2,128]{3,1,2,0:T(8,128)(2,1)} copy(bf16[64,8,2,128]{3,2,1,0:T(2,128)(2,1)S(1)} %bitcast.18) | data formatting | bytes 524288
  43.9 0.7 %pad_add_fusion.order_ref = s32[5]{0:T(128)} fusion(s32[1]{0:T(128)} %bitcast, s32[4]{0:T(128)S(1)} %iota_xor_fusion), kind=kLoop, calls=%fused_computation.7 | loop fusion | flops 5 | bytes 40 | tf_op jit(solution)/shard_map/concatenate | solution.py:160
  44.6 0.0 collective-permute-done.4.refs_3_
  44.6 0.0 copy-start.2
  44.6 0.1 collective-permute-done.1.refs_1_
  44.7 0.0 copy-start.3
  44.7 0.0 copy-done
  44.7 0.0 copy-done.1
  44.7 0.7 %copy-done.2 = bf16[4,2,288,128]{3,2,1,0:T(8,128)(2,1)} copy-done((bf16[4,2,288,128]{3,2,1,0:T(8,128)(2,1)}, bf16[4,2,288,128]{3,2,1,0:T(8,128)(2,1)S(1)}, u32[]{:S(2)}) %copy-start.2) | copy-done | bytes 589848
  45.4 0.2 copy-done.3
  45.6 6.2 %expand.1 = (bf16[1,2,192,2048]{3,2,1,0:T(8,128)(2,1)}, bf16[4096,128]{1,0:T(8,128)(2,1)}) custom-call(s32[5]{0:T(128)} %pad_add_fusion.order_ref, bf16[4,2,288,128]{3,2,1,0:T(8,128)(2,1)} %bitcast.12, bf16[4,2,288,128]{3,2,1,0:T(8,128)(2,1)} %copy-done.3, bf16[4,2,288,128]{3,2,1,0:T(8,128)(2,1)} %bitcast.14, bf16[4,2,288,128]{3,2,1,0:T(8,128)(2,1)} %copy-done.2, ...), custom_call_target="tpu_custom_call" | custom-call | tf_op jit(solution)/shard_map/expand/pallas_call | solution.py:120
  (3 shorter events, 0.0 us)
Async XLA Ops:
  0.7 41.7 %copy-start.4 = (bf16[512,2,128]{2,1,0:T(2,128)(2,1)S(1)}, bf16[512,2,128]{2,1,0:T(2,128)(2,1)}, u32[]{:S(2)}) copy-start(bf16[512,2,128]{2,1,0:T(2,128)(2,1)} %param.8) | copy-start | bytes 786436
  2.6 40.6 %copy-start.5 = (bf16[512,2,128]{2,1,0:T(2,128)(2,1)S(1)}, bf16[512,2,128]{2,1,0:T(2,128)(2,1)}, u32[]{:S(2)}) copy-start(bf16[512,2,128]{2,1,0:T(2,128)(2,1)} %param.9) | copy-start | bytes 786436
  3.7 5.6 %collective-permute-start = (bf16[1,288,128]{2,1,0:T(8,128)(2,1)S(1)}, bf16[1,288,128]{2,1,0:T(8,128)(2,1)S(1)}, u32[]{:S(2)}, u32[]{:S(2)}) collective-permute-start(bf16[1,288,128]{2,1,0:T(8,128)(2,1)S(1)} %get-tuple-element.10), channel_id=1, source_target_pairs={{0,8},{8,0},{16,24},{24,16},{1,9},{9,1},{17,25},{25,17},{2,10},{10... | collective-permute-start | bytes 221192 | tf_op jit(solution)/shard_map/ppermute | solution.py:159
  6.7 18.8 %collective-permute-start.2 = (bf16[1,288,128]{2,1,0:T(8,128)(2,1)S(1)}, bf16[1,288,128]{2,1,0:T(8,128)(2,1)S(1)}, u32[]{:S(2)}, u32[]{:S(2)}) collective-permute-start(bf16[1,288,128]{2,1,0:T(8,128)(2,1)S(1)} %get-tuple-element.8), channel_id=1, source_target_pairs={{0,16},{8,24},{16,0},{24,8},{1,17},{9,25},{17,1},{25,9},{2,18},{10... | collective-permute-start | bytes 221192 | tf_op jit(solution)/shard_map/ppermute | solution.py:159
  8.2 17.3 %collective-permute-start.3 = (bf16[1,288,128]{2,1,0:T(8,128)(2,1)S(1)}, bf16[1,288,128]{2,1,0:T(8,128)(2,1)S(1)}, u32[]{:S(2)}, u32[]{:S(2)}) collective-permute-start(bf16[1,288,128]{2,1,0:T(8,128)(2,1)S(1)} %get-tuple-element.9), channel_id=1, source_target_pairs={{0,24},{8,16},{16,8},{24,0},{1,25},{9,17},{17,9},{25,1},{2,26},{10... | collective-permute-start | bytes 221192 | tf_op jit(solution)/shard_map/ppermute | solution.py:159
  25.5 19.2 %copy-start = (bf16[8,288,128]{2,1,0:T(8,128)(2,1)}, bf16[8,288,128]{2,1,0:T(8,128)(2,1)S(1)}, u32[]{:S(2)}) copy-start(bf16[8,288,128]{2,1,0:T(8,128)(2,1)S(1)} %all-gather) | copy-start | bytes 1769476
  41.8 2.9 %copy-start.1 = (bf16[8,288,128]{2,1,0:T(8,128)(2,1)}, bf16[8,288,128]{2,1,0:T(8,128)(2,1)S(1)}, u32[]{:S(2)}) copy-start(bf16[8,288,128]{2,1,0:T(8,128)(2,1)S(1)} %all-gather.1) | copy-start | bytes 1769476
  41.8 2.8 %collective-permute-start.4 = (bf16[4,2,288,128]{3,2,1,0:T(8,128)(2,1)S(1)}, bf16[4,2,288,128]{3,2,1,0:T(8,128)(2,1)S(1)}, u32[]{:S(2)}, u32[]{:S(2)}) collective-permute-start(bf16[4,2,288,128]{3,2,1,0:T(8,128)(2,1)S(1)} %bitcast.13), channel_id=1, source_target_pairs={{0,1},{1,0},{2,3},{3,2},{4,5},{5,4},{6,7},{7,6},{8,9},{9,8},{10,11... | collective-permute-start | bytes 1769480 | tf_op jit(solution)/shard_map/ppermute | solution.py:174
  41.8 2.8 %collective-permute-start.1 = (bf16[4,2,288,128]{3,2,1,0:T(8,128)(2,1)S(1)}, bf16[4,2,288,128]{3,2,1,0:T(8,128)(2,1)S(1)}, u32[]{:S(2)}, u32[]{:S(2)}) collective-permute-start(bf16[4,2,288,128]{3,2,1,0:T(8,128)(2,1)S(1)} %bitcast.11), channel_id=1, source_target_pairs={{0,1},{1,0},{2,3},{3,2},{4,5},{5,4},{6,7},{7,6},{8,9},{9,8},{10,11... | collective-permute-start | bytes 1769480 | tf_op jit(solution)/shard_map/ppermute | solution.py:174
  44.6 0.8 %copy-start.2 = (bf16[4,2,288,128]{3,2,1,0:T(8,128)(2,1)}, bf16[4,2,288,128]{3,2,1,0:T(8,128)(2,1)S(1)}, u32[]{:S(2)}) copy-start(bf16[4,2,288,128]{3,2,1,0:T(8,128)(2,1)S(1)} %collective-permute-done.4.refs_3_) | copy-start | bytes 1769476
  44.7 1.0 %copy-start.3 = (bf16[4,2,288,128]{3,2,1,0:T(8,128)(2,1)}, bf16[4,2,288,128]{3,2,1,0:T(8,128)(2,1)S(1)}, u32[]{:S(2)}) copy-start(bf16[4,2,288,128]{3,2,1,0:T(8,128)(2,1)S(1)} %collective-permute-done.1.refs_1_) | copy-start | bytes 1769476

commit v2 on v1

--- a/solution.py
+++ b/solution.py
@@ -5,37 +5,157 @@
 from jax.experimental.pallas import tpu as pltpu
 from jax.sharding import PartitionSpec as P
 
+
 LANES = 128
-CHUNKS = 2
-
-
-def pack_rows(latents, rotary, latent_gain):
-    seqs, count, width = latents.shape
+CORES = 2
+CHUNKS = 1
+VMEM = pl.BlockSpec(memory_space=pltpu.VMEM)
+HBM = pl.BlockSpec(memory_space=pl.ANY)
+
+
+def pack_rows(latents, rotary, latent_gain, spans):
+    _, count, width = latents.shape
     rot = rotary.shape[2]
     fold = LANES // rot
     pieces = width // LANES
     high = pieces * count + count // fold
-
-    def body(rows_ref, rotary_ref, gain_ref, out_ref):
-        for s in range(seqs):
-            rows = rows_ref[s].astype(jnp.float32)
+    cut = count // fold
+
+    def body(rows_ref, rotary_ref, gain_ref, *outs):
+        me = lax.axis_index("span")
+        for k in range(spans):
+            rows = rows_ref[me ^ k].astype(jnp.float32)
             scale = lax.rsqrt(jnp.mean(rows * rows, axis=-1, keepdims=True) + 1e-06)
             ready = (rows * scale * gain_ref[...]).astype(jnp.bfloat16)
             for i in range(pieces):
-                out_ref[s, i * count : (i + 1) * count] = ready[:, i * LANES : (i + 1) * LANES]
-            part = rotary_ref[s].astype(jnp.float32)
-            cut = count // fold
+                outs[k][0, i * count : (i + 1) * count] = ready[:, i * LANES : (i + 1) * LANES]
+            part = rotary_ref[me ^ k].astype(jnp.float32)
             wide = jnp.concatenate([part[i * cut : (i + 1) * cut] for i in range(fold)], axis=1)
-            out_ref[s, pieces * count :] = wide.astype(jnp.bfloat16)
+            outs[k][0, pieces * count :] = wide.astype(jnp.bfloat16)
 
     return pl.pallas_call(
         body,
-        out_shape=jax.ShapeDtypeStruct((seqs, high, LANES), jnp.bfloat16),
+        in_specs=[VMEM] * 3,
+        out_specs=[VMEM] * spans,
+        out_shape=[jax.ShapeDtypeStruct((1, high, LANES), jnp.bfloat16)] * spans,
         name="pack",
     )(latents, rotary, latent_gain.reshape(1, -1))
 
 
-def expand(order, chunks, keys_t, values, count, rot, width, spans, core):
+def expand(slots, before, keys_t, values, shape, last):
+    heads, key_part, value_size, count, rot, width, spans, zs = shape
+    pieces, fold = width // LANES, LANES // rot
+    cut = count // fold
+    tile = CORES * count
+    every = spans * tile
+    arrays = [a for _, chunks in slots for pair in chunks for a in pair]
+    count_in = len(arrays) + 2 + len(before)
+
+    def body(*refs):
+        ins, keys_ref, value_ref = refs[: len(arrays)], refs[len(arrays)], refs[len(arrays) + 1]
+        keys_out, values_out, rows_s, rot_s, wide_s, key_s, value_s, sems = refs[count_in:]
+        me, place = lax.axis_index("span"), lax.axis_index("model")
+        z, first = place // CORES, (place % CORES) == 0
+
+        def block(s, k):
+            return (me ^ k) * zs + z + slots[s][0]
+
+        def key_copies(s):
+            for k in range(spans):
+                at = pl.multiple_of(block(s, k) * tile, tile)
+                to = keys_out.at[0, :, :, pl.ds(at, tile)]
+                yield pltpu.make_async_copy(key_s.at[s, k], to, sems.at[s, k, 0])
+
+        def value_copies(s):
+            for k in range(spans):
+                at = pl.multiple_of(block(s, k) * tile * heads, tile * heads)
+                to = values_out.at[pl.ds(at, tile * heads)]
+                yield pltpu.make_async_copy(value_s.at[s, k], to, sems.at[s, k, 1])
+
+        def work(s, base):
+            k = 0
+            for j, chunk in enumerate(slots[s][1]):
+                own, other = ins[base + 2 * j], ins[base + 2 * j + 1]
+                for b in range(chunk[0].shape[0]):
+                    mine, theirs = own[b], other[b]
+                    got = (jnp.where(first, mine, theirs), jnp.where(first, theirs, mine))
+                    for c in range(CORES):
+                        at = (k * CORES + c) * count
+                        for i in range(pieces):
+                            rows_s[at : at + count, i * LANES : (i + 1) * LANES] = got[c][
+                                i * count : (i + 1) * count
+                            ]
+                        tail = got[c][pieces * count :].astype(jnp.float32)
+                        for i in range(fold):
+                            rot_s[at + i * cut : at + (i + 1) * cut] = tail[
+                                :, i * rot : (i + 1) * rot
+                            ].astype(jnp.bfloat16)
+                    k += 1
+            rows = rows_s[...]
+            dims = (((1,), (1,)), ((), ()))
+            wide_keys = lax.dot_general(keys_ref[...], rows, dims, preferred_element_type=jnp.float32)
+            wide_keys = wide_keys.astype(jnp.bfloat16)
+            eye = (
+                lax.broadcasted_iota(jnp.int32, (rot, rot), 0)
+                == lax.broadcasted_iota(jnp.int32, (rot, rot), 1)
+            ).astype(jnp.float32).astype(jnp.bfloat16)
+            shared = lax.dot_general(eye, rot_s[...], dims, preferred_element_type=jnp.float32)
+            shared = shared.astype(jnp.bfloat16)
+            for k in range(spans):
+                lanes = slice(k * tile, (k + 1) * tile)
+                for h in range(heads):
+                    key_s[s, k, h, :key_part] = wide_keys[h * key_part : (h + 1) * key_part, lanes]
+                    key_s[s, k, h, key_part:] = shared[:, lanes]
+            for copy in key_copies(s):
+                copy.start()
+            wide_values = jnp.dot(rows, value_ref[...], preferred_element_type=jnp.float32)
+            for h in range(heads):
+                wide_s[pl.ds(h, every, stride=heads)] = wide_values[
+                    :, h * value_size : (h + 1) * value_size
+                ]
+            for k in range(spans):
+                value_s[s, k] = wide_s[k * tile * heads : (k + 1) * tile * heads].astype(jnp.bfloat16)
+            for copy in value_copies(s):
+                copy.start()
+
+        base = 0
+        for s, (offset, chunks) in enumerate(slots):
+            there = (z + offset >= 0) & (z + offset < zs)
+            pl.when(there)(lambda s=s, base=base: work(s, base))
+            base += 2 * len(chunks)
+        for s, (offset, _) in enumerate(slots):
+            there = (z + offset >= 0) & (z + offset < zs)
+
+            @pl.when(there)
+            def _(s=s):
+                for copy in (*key_copies(s), *value_copies(s)):
+                    copy.wait()
+
+    length = every * zs
+    given = (*arrays, keys_t, values)
+    if last:
+        given = [pltpu.with_memory_space_constraint(a, pltpu.VMEM) for a in given]
+    return pl.pallas_call(
+        body,
+        in_specs=[VMEM] * (len(arrays) + 2) + [HBM] * len(before),
+        out_specs=[HBM, HBM],
+        out_shape=[
+            jax.ShapeDtypeStruct((1, heads, key_part + rot, length), jnp.bfloat16),
+            jax.ShapeDtypeStruct((length * heads, value_size), jnp.bfloat16),
+        ],
+        scratch_shapes=[
+            pltpu.VMEM((every, width), jnp.bfloat16),
+            pltpu.VMEM((every, rot), jnp.bfloat16),
+            pltpu.VMEM((every * heads, value_size), jnp.float32),
+            pltpu.VMEM((len(slots), spans, heads, key_part + rot, tile), jnp.bfloat16),
+            pltpu.VMEM((len(slots), spans, tile * heads, value_size), jnp.bfloat16),
+            pltpu.SemaphoreType.DMA((len(slots), spans, 2)),
+        ],
+        input_output_aliases={len(arrays) + 2 + i: i for i in range(len(before))},
+    )(*given, *before)
+
+
+def expand_spans(order, chunks, keys_t, values, count, rot, width, spans):
     heads = values.shape[1]
     key_part = keys_t.shape[0] // heads
     value_size = values.shape[2]
@@ -138,41 +258,64 @@
             jax.ShapeDtypeStruct((1, heads, key_part + rot, length), jnp.bfloat16),
             jax.ShapeDtypeStruct((length * heads, value_size), jnp.bfloat16),
         ],
-        name="expand",
+        name="expand_spans",
     )(order, *[a for chunk in chunks for a in chunk], keys_t, values)
     return decode_keys, decode_values.reshape(1, length, heads, value_size)
 
 
-def shards(latents, rotary_rows, latent_gain, key_up, value_up):
+def decode(latents, rotary_rows, latent_gain, key_up, value_up):
     spans, models = lax.axis_size("span"), lax.axis_size("model")
-    me, place = lax.axis_index("span"), lax.axis_index("model")
+    zs = models // CORES
     _, count, width = latents.shape
     rot = rotary_rows.shape[2]
-    cores = 2
-    core = place % cores
-    packed = pack_rows(latents, rotary_rows, latent_gain)
+    heads, key_part, value_size = key_up.shape[1], key_up.shape[2], value_up.shape[2]
+    shape = (heads, key_part, value_size, count, rot, width, spans, zs)
+    packed = pack_rows(latents, rotary_rows, latent_gain, spans)
     keys_t = key_up.transpose(1, 2, 0).reshape(-1, width)
-
-    parts = [lax.dynamic_slice_in_dim(packed, me, 1, 0)]
+    values = value_up.reshape(width, heads * value_size)
+    swap = [(i, i ^ 1) for i in range(models)]
+
+    parts = [packed[0]]
     for k in range(1, spans):
-        sent = lax.dynamic_slice_in_dim(packed, me ^ k, 1, 0)
-        parts.append(lax.ppermute(sent, "span", [(i, i ^ k) for i in range(spans)]))
-    order = jnp.concatenate(
-        [me ^ jnp.arange(spans, dtype=jnp.int32), core.astype(jnp.int32)[None]]
-    )
-
-    along = [[z * cores + c for z in range(models // cores)] for c in range(cores)]
-    swap = [(i, i ^ 1) for i in range(models)]
-    chunks, size = [], spans // CHUNKS
-    token = None
-    for j in range(CHUNKS):
-        mine = jnp.concatenate(parts[j * size : (j + 1) * size], axis=0)
-        if token is not None:
-            mine, _ = lax.optimization_barrier((mine, token))
+        parts.append(lax.ppermute(packed[k], "span", [(i, i ^ k) for i in range(spans)]))
+    size = spans // CHUNKS
+    keys_t, values, *parts[1:] = lax.optimization_barrier((keys_t, values, *parts[1:]))
+    if (CORES * count) % LANES:
+        me, place = lax.axis_index("span"), lax.axis_index("model")
+        core = place % CORES
+        order = jnp.concatenate(
+            [me ^ jnp.arange(spans, dtype=jnp.int32), core.astype(jnp.int32)[None]]
+        )
+        along = [[z * CORES + c for z in range(zs)] for c in range(CORES)]
+        mine = jnp.concatenate(parts, axis=0)
         own = lax.all_gather(mine, "model", axis_index_groups=along)
-        token = own
-        chunks.append((own, lax.ppermute(own, "model", swap)))
-    return expand(order, chunks, keys_t, value_up, count, rot, width, spans, core)
+        chunks = [(own, lax.ppermute(own, "model", swap))]
+        return expand_spans(order, chunks, keys_t, value_up, count, rot, width, spans)
+    own = [jnp.concatenate(parts[j * size : (j + 1) * size], axis=0) for j in range(CHUNKS)]
+
+    def hop(x, way, far):
+        pairs = []
+        for z in range(zs):
+            if 0 <= z + way < zs and 0 <= z - way * far < zs:
+                for c in range(CORES):
+                    pairs.append((z * CORES + c, (z + way) * CORES + c))
+        return lax.ppermute(x, "model", pairs)
+
+    def paired(x):
+        return (x, lax.ppermute(x, "model", swap))
+
+    slots = [[(0, [paired(x) for x in own])]]
+    moving = {1: own, -1: own}
+    for d in range(1, zs):
+        for way in (1, -1):
+            moving[way] = [hop(x, way, d - 1) for x in moving[way]]
+        slots.append([(-way * d, [paired(x) for x in moving[way]]) for way in (1, -1)])
+    groups = [sum(slots[:-1], []), slots[-1]]
+    outs = ()
+    for n, group in enumerate(groups):
+        outs = expand(group, outs, keys_t, values, shape, n == 1)
+    decode_keys, decode_values = outs
+    return decode_keys, decode_values.reshape(1, -1, heads, value_size)
 
 
 def solution(mesh):
@@ -184,7 +327,7 @@
         P(None, "model", None),
     )
     return jax.shard_map(
-        shards,
+        decode,
         mesh=mesh,
         in_specs=placed,
         out_specs=(P("span", "model", None, None), P("span", None, "model", None)),

time: 52.1 us -> 48.7 us (0.935)
  the two profiles are of different devices: /device:TPU:0 before, /device:TPU:27 now
where the time goes in v2:
time: 48.7 us; the launch traced here: 48.3 us
  starting transfers between devices  22 us (45%)
  waiting for transfers between devices  11.1 us (23%)
  Pallas kernels  8.21 us (17%)
  local copies, waits for them, and re-layouts  6.19 us (13%)
  between operations  0.82 us (2%)
    ppermute x7, starting transfers between devices, paired(): return (x, lax.ppermute(x, 'model', swap))  12 us
    ppermute x6, waiting for transfers between devices, hop(): return lax.ppermute(x, 'model', pairs)  11.1 us
    ppermute x6, starting transfers between devices, hop(): return lax.ppermute(x, 'model', pairs)  7.41 us
    pallas_call x2, Pallas kernels, expand(): pl.pallas_call(body, in_specs=[VMEM] * (len(arrays) + 2) + [HBM] * len(be...  6.4 us
    unnamed x26, local copies, waits for them, and re-layouts  4.36 us
    ppermute x3, starting transfers between devices, decode(): lax.ppermute(packed[k], 'span', [(i, i ^ k) for i in range(spans)])  2.65 us
    transpose x1, local copies, waits for them, and re-layouts, decode(): keys_t = key_up.transpose(1, 2, 0).reshape(-1, width)  1.82 us
    pallas_call x1, Pallas kernels, pack_rows(): pl.pallas_call(body, in_specs=[VMEM] * 3, out_specs=[VMEM] * spans, out_s...  1.81 us
  transfers between devices with their start and end apart: 16, of which 4 were waited for; matrix products, arithmetic and copies ran while one was open for 9% of the time, Pallas kernels for 10%

profile of v2, /device:TPU:27, one launch (start us, length us, event | category | flops | bytes accessed | tf_op | source)
XLA Modules:
  0.0 48.3 jit_solution(834068766355005077)
XLA Ops:
  0.6 1.8 %pack.1 = (bf16[1,288,128]{2,1,0:T(8,128)(2,1)}, bf16[1,288,128]{2,1,0:T(8,128)(2,1)}, bf16[1,288,128]{2,1,0:T(8,128)(2,1)}, bf16[1,288,128]{2,1,0:T(8,128)(2,1)}) custom-call(bf16[4,64,512]{2,1,0:T(8,128)(2,1)} %rows_ref.1, bf16[4,64,64]{2,1,0:T(8,128)(2,1)} %rotary_ref.1, f32[1,512]{1,0:T(1,128)} %bitcast.15), custom_call_target="tpu_custom_call" | custom-call | tf_op jit(solution)/shard_map/pack/pallas_call | solution.py:36
  2.4 0.3 collective-permute-start
  2.7 1.2 %collective-permute-start.1 = (bf16[1,288,128]{2,1,0:T(8,128)(2,1)}, bf16[1,288,128]{2,1,0:T(8,128)(2,1)S(1)}, u32[]{:S(2)}, u32[]{:S(2)}) collective-permute-start(bf16[1,288,128]{2,1,0:T(8,128)(2,1)} %get-tuple-element.17), channel_id=1, source_target_pairs={{0,16},{8,24},{16,0},{24,8},{1,17},{9,25},{17,1},{25,9},{2,18},{10... | collective-permute-start | bytes 221192 | tf_op jit(solution)/shard_map/ppermute | solution.py:280
  3.9 1.2 %collective-permute-start.2 = (bf16[1,288,128]{2,1,0:T(8,128)(2,1)}, bf16[1,288,128]{2,1,0:T(8,128)(2,1)S(1)}, u32[]{:S(2)}, u32[]{:S(2)}) collective-permute-start(bf16[1,288,128]{2,1,0:T(8,128)(2,1)} %get-tuple-element.18), channel_id=1, source_target_pairs={{0,24},{8,16},{16,8},{24,0},{1,25},{9,17},{17,9},{25,1},{2,26},{10... | collective-permute-start | bytes 221192 | tf_op jit(solution)/shard_map/ppermute | solution.py:280
  5.1 1.8 %copy.9 = bf16[2,128,512]{2,1,0:T(8,128)(2,1)} copy(bf16[2,128,512]{1,0,2:T(2,128)(2,1)} %bitcast.13) | data formatting | bytes 524288 | tf_op jit(solution)/shard_map/transpose | solution.py:274
  6.9 1.7 %copy.12 = bf16[64,8,2,128]{3,1,2,0:T(8,128)(2,1)} copy(bf16[64,8,2,128]{3,2,1,0:T(2,128)(2,1)} %bitcast.14) | data formatting | bytes 524288
  8.6 0.9 %constant_dynamic-update-slice_fusion.3 = bf16[4,288,128]{2,1,0:T(8,128)(2,1)S(1)} fusion(bf16[1,288,128]{2,1,0:T(8,128)(2,1)} %get-tuple-element.15), kind=kLoop, calls=%fused_computation.4 | loop fusion | bytes 147456
  9.5 0.0 collective-permute-done.2
  9.6 2.2 %collective-permute-start.7 = (bf16[4,288,128]{2,1,0:T(8,128)(2,1)S(1)}, bf16[4,288,128]{2,1,0:T(8,128)(2,1)S(1)}, u32[]{:S(2)}, u32[]{:S(2)}) collective-permute-start(bf16[4,288,128]{2,1,0:T(8,128)(2,1)S(1)} %constant_dynamic-update-slice_fusion.refs_0_), channel_id=1, source_target_pairs={{2,0},{3,1},{4,2},{5,3},{6,4},{7,5},{10,8},{11,9},{12,10},{13,11},... | collective-permute-start | bytes 884744 | tf_op jit(solution)/shard_map/ppermute | solution.py:302
  11.8 1.3 %collective-permute-start.3 = (bf16[4,288,128]{2,1,0:T(8,128)(2,1)S(1)}, bf16[4,288,128]{2,1,0:T(8,128)(2,1)S(1)}, u32[]{:S(2)}, u32[]{:S(2)}) collective-permute-start(bf16[4,288,128]{2,1,0:T(8,128)(2,1)S(1)} %constant_dynamic-update-slice_fusion.refs_0_), channel_id=1, source_target_pairs={{0,2},{1,3},{2,4},{3,5},{4,6},{5,7},{8,10},{9,11},{10,12},{11,13},... | collective-permute-start | bytes 884744 | tf_op jit(solution)/shard_map/ppermute | solution.py:302
  13.1 3.5 %collective-permute-done.7.refs_4_ = bf16[4,288,128]{2,1,0:T(8,128)(2,1)S(1)} collective-permute-done((bf16[4,288,128]{2,1,0:T(8,128)(2,1)S(1)}, bf16[4,288,128]{2,1,0:T(8,128)(2,1)S(1)}, u32[]{:S(2)}, u32[]{:S(2)}) %collective-permute-start.7) | collective-permute-done | bytes 294944 | tf_op jit(solution)/shard_map/ppermute | solution.py:302
  16.6 0.7 %collective-permute-start.8 = (bf16[4,288,128]{2,1,0:T(8,128)(2,1)S(1)}, bf16[4,288,128]{2,1,0:T(8,128)(2,1)S(1)}, u32[]{:S(2)}, u32[]{:S(2)}) collective-permute-start(bf16[4,288,128]{2,1,0:T(8,128)(2,1)S(1)} %collective-permute-done.7.refs_4_), channel_id=1, source_target_pairs={{2,0},{3,1},{4,2},{5,3},{10,8},{11,9},{12,10},{13,11},{18,16},{19,... | collective-permute-start | bytes 884744 | tf_op jit(solution)/shard_map/ppermute | solution.py:302
  17.3 3.2 %collective-permute-done.3.refs_2_ = bf16[4,288,128]{2,1,0:T(8,128)(2,1)S(1)} collective-permute-done((bf16[4,288,128]{2,1,0:T(8,128)(2,1)S(1)}, bf16[4,288,128]{2,1,0:T(8,128)(2,1)S(1)}, u32[]{:S(2)}, u32[]{:S(2)}) %collective-permute-start.3) | collective-permute-done | bytes 294944 | tf_op jit(solution)/shard_map/ppermute | solution.py:302
  20.5 1.3 %collective-permute-start.4 = (bf16[4,288,128]{2,1,0:T(8,128)(2,1)S(1)}, bf16[4,288,128]{2,1,0:T(8,128)(2,1)S(1)}, u32[]{:S(2)}, u32[]{:S(2)}) collective-permute-start(bf16[4,288,128]{2,1,0:T(8,128)(2,1)S(1)} %collective-permute-done.3.refs_2_), channel_id=1, source_target_pairs={{2,4},{3,5},{4,6},{5,7},{10,12},{11,13},{12,14},{13,15},{18,20},{1... | collective-permute-start | bytes 884744 | tf_op jit(solution)/shard_map/ppermute | solution.py:302
  21.8 2.7 %collective-permute-start.11 = (bf16[4,288,128]{2,1,0:T(8,128)(2,1)S(1)}, bf16[4,288,128]{2,1,0:T(8,128)(2,1)S(1)}, u32[]{:S(2)}, u32[]{:S(2)}) collective-permute-start(bf16[4,288,128]{2,1,0:T(8,128)(2,1)S(1)} %constant_dynamic-update-slice_fusion.refs_0_), channel_id=1, source_target_pairs={{0,1},{1,0},{2,3},{3,2},{4,5},{5,4},{6,7},{7,6},{8,9},{9,8},{10,11... | collective-permute-start | bytes 884744 | tf_op jit(solution)/shard_map/ppermute | solution.py:305
  24.5 0.1 collective-permute-start.13
  24.6 0.7 %collective-permute-start.9 = (bf16[4,288,128]{2,1,0:T(8,128)(2,1)S(1)}, bf16[4,288,128]{2,1,0:T(8,128)(2,1)S(1)}, u32[]{:S(2)}, u32[]{:S(2)}) collective-permute-start(bf16[4,288,128]{2,1,0:T(8,128)(2,1)S(1)} %collective-permute-done.8.refs_8_), channel_id=1, source_target_pairs={{2,0},{3,1},{10,8},{11,9},{18,16},{19,17},{26,24},{27,25}} | collective-permute-start | bytes 884744 | tf_op jit(solution)/shard_map/ppermute | solution.py:302
  25.2 3.0 %collective-permute-done.4.refs_6_ = bf16[4,288,128]{2,1,0:T(8,128)(2,1)S(1)} collective-permute-done((bf16[4,288,128]{2,1,0:T(8,128)(2,1)S(1)}, bf16[4,288,128]{2,1,0:T(8,128)(2,1)S(1)}, u32[]{:S(2)}, u32[]{:S(2)}) %collective-permute-start.4) | collective-permute-done | bytes 294944 | tf_op jit(solution)/shard_map/ppermute | solution.py:302
  28.3 1.3 %collective-permute-start.5 = (bf16[4,288,128]{2,1,0:T(8,128)(2,1)S(1)}, bf16[4,288,128]{2,1,0:T(8,128)(2,1)S(1)}, u32[]{:S(2)}, u32[]{:S(2)}) collective-permute-start(bf16[4,288,128]{2,1,0:T(8,128)(2,1)S(1)} %collective-permute-done.4.refs_6_), channel_id=1, source_target_pairs={{4,6},{5,7},{12,14},{13,15},{20,22},{21,23},{28,30},{29,31}} | collective-permute-start | bytes 884744 | tf_op jit(solution)/shard_map/ppermute | solution.py:302
  29.6 3.6 %collective-permute-start.12 = (bf16[4,288,128]{2,1,0:T(8,128)(2,1)S(1)}, bf16[4,288,128]{2,1,0:T(8,128)(2,1)S(1)}, u32[]{:S(2)}, u32[]{:S(2)}) collective-permute-start(bf16[4,288,128]{2,1,0:T(8,128)(2,1)S(1)} %collective-permute-done.3.refs_2_), channel_id=1, source_target_pairs={{0,1},{1,0},{2,3},{3,2},{4,5},{5,4},{6,7},{7,6},{8,9},{9,8},{10,11... | collective-permute-start | bytes 884744 | tf_op jit(solution)/shard_map/ppermute | solution.py:305
  33.1 0.0 collective-permute-done.11.refs_1_
  33.1 0.1 collective-permute-start.15
  33.2 0.4 collective-permute-start.14
  33.7 0.3 copy-done.8
  34.0 0.0 collective-permute-done.9.refs_2_
  34.0 0.4 collective-permute-start.10
  34.4 1.3 %collective-permute-done.5.refs_0_ = bf16[4,288,128]{2,1,0:T(8,128)(2,1)S(1)} collective-permute-done((bf16[4,288,128]{2,1,0:T(8,128)(2,1)S(1)}, bf16[4,288,128]{2,1,0:T(8,128)(2,1)S(1)}, u32[]{:S(2)}, u32[]{:S(2)}) %collective-permute-start.5) | collective-permute-done | bytes 294944 | tf_op jit(solution)/shard_map/ppermute | solution.py:302
  35.7 4.7 %collective-permute-start.6 = (bf16[4,288,128]{2,1,0:T(8,128)(2,1)S(1)}, bf16[4,288,128]{2,1,0:T(8,128)(2,1)S(1)}, u32[]{:S(2)}, u32[]{:S(2)}) collective-permute-start(bf16[4,288,128]{2,1,0:T(8,128)(2,1)S(1)} %collective-permute-done.5.refs_0_), channel_id=1, source_target_pairs={{0,1},{1,0},{2,3},{3,2},{4,5},{5,4},{6,7},{7,6},{8,9},{9,8},{10,11... | collective-permute-start | bytes 884744 | tf_op jit(solution)/shard_map/ppermute | solution.py:305
  40.4 0.7 %copy-done.9 = bf16[4,288,128]{2,1,0:T(8,128)(2,1)} copy-done((bf16[4,288,128]{2,1,0:T(8,128)(2,1)}, bf16[4,288,128]{2,1,0:T(8,128)(2,1)S(1)}, u32[]{:S(2)}) %copy-start.9) | copy-done | bytes 294936
  41.1 0.7 %copy-done.10 = bf16[4,288,128]{2,1,0:T(8,128)(2,1)} copy-done((bf16[4,288,128]{2,1,0:T(8,128)(2,1)}, bf16[4,288,128]{2,1,0:T(8,128)(2,1)S(1)}, u32[]{:S(2)}) %copy-start.10) | copy-done | bytes 294936
  41.9 4.9 %shard_map.68 = (bf16[1,2,192,2048]{3,2,1,0:T(8,128)(2,1)}, bf16[4096,128]{1,0:T(8,128)(2,1)}) custom-call(bf16[4,288,128]{2,1,0:T(8,128)(2,1)} %copy-done.2, bf16[4,288,128]{2,1,0:T(8,128)(2,1)} %copy-done.7, bf16[4,288,128]{2,1,0:T(8,128)(2,1)} %copy-done.4, bf16[4,288,128]{2,1,0:T(8,128)(2,1)} %copy-done.9, bf16[4,288,128]{2,1,0:T(8,128)(2,1)} %copy-done.3, ...), custom_call_target="tpu_custom_call" | custom-call | tf_op jit(solution)/shard_map/pallas_call | solution.py:138
  46.8 1.5 %shard_map.69 = (bf16[1,2,192,2048]{3,2,1,0:T(8,128)(2,1)}, bf16[4096,128]{1,0:T(8,128)(2,1)}) custom-call(bf16[4,288,128]{2,1,0:T(8,128)(2,1)S(1)} %collective-permute-done.5.refs_0_, bf16[4,288,128]{2,1,0:T(8,128)(2,1)S(1)} %collective-permute-done.6.refs_1_, ...), custom_call_target="tpu_custom_call", output_to_operand_aliasing={{0}: (6, {}), {1}: (7, {})} | custom-call | tf_op jit(solution)/shard_map/pallas_call | solution.py:138
  (31 shorter events, 0.1 us)
Async XLA Ops:
  2.4 7.0 %collective-permute-start = (bf16[1,288,128]{2,1,0:T(8,128)(2,1)}, bf16[1,288,128]{2,1,0:T(8,128)(2,1)S(1)}, u32[]{:S(2)}, u32[]{:S(2)}) collective-permute-start(bf16[1,288,128]{2,1,0:T(8,128)(2,1)} %get-tuple-element.16), channel_id=1, source_target_pairs={{0,8},{8,0},{16,24},{24,16},{1,9},{9,1},{17,25},{25,17},{2,10},{10... | collective-permute-start | bytes 221192 | tf_op jit(solution)/shard_map/ppermute | solution.py:280
  2.7 6.8 %collective-permute-start.1 = (bf16[1,288,128]{2,1,0:T(8,128)(2,1)}, bf16[1,288,128]{2,1,0:T(8,128)(2,1)S(1)}, u32[]{:S(2)}, u32[]{:S(2)}) collective-permute-start(bf16[1,288,128]{2,1,0:T(8,128)(2,1)} %get-tuple-element.17), channel_id=1, source_target_pairs={{0,16},{8,24},{16,0},{24,8},{1,17},{9,25},{17,1},{25,9},{2,18},{10... | collective-permute-start | bytes 221192 | tf_op jit(solution)/shard_map/ppermute | solution.py:280
  3.9 5.5 %collective-permute-start.2 = (bf16[1,288,128]{2,1,0:T(8,128)(2,1)}, bf16[1,288,128]{2,1,0:T(8,128)(2,1)S(1)}, u32[]{:S(2)}, u32[]{:S(2)}) collective-permute-start(bf16[1,288,128]{2,1,0:T(8,128)(2,1)} %get-tuple-element.18), channel_id=1, source_target_pairs={{0,24},{8,16},{16,8},{24,0},{1,25},{9,17},{17,9},{25,1},{2,26},{10... | collective-permute-start | bytes 221192 | tf_op jit(solution)/shard_map/ppermute | solution.py:280
  9.5 32.3 %copy-start.2 = (bf16[4,288,128]{2,1,0:T(8,128)(2,1)}, bf16[4,288,128]{2,1,0:T(8,128)(2,1)S(1)}, u32[]{:S(2)}) copy-start(bf16[4,288,128]{2,1,0:T(8,128)(2,1)S(1)} %constant_dynamic-update-slice_fusion.refs_0_) | copy-start | bytes 884740
  9.6 37.3 %copy-start = (bf16[2,128,512]{2,1,0:T(8,128)(2,1)S(1)}, bf16[2,128,512]{2,1,0:T(8,128)(2,1)}, u32[]{:S(2)}) copy-start(bf16[2,128,512]{2,1,0:T(8,128)(2,1)} %copy.9) | copy-start | bytes 786436
  9.6 37.3 %copy-start.1 = (bf16[64,8,2,128]{3,1,2,0:T(8,128)(2,1)S(1)}, bf16[64,8,2,128]{3,1,2,0:T(8,128)(2,1)}, u32[]{:S(2)}) copy-start(bf16[64,8,2,128]{3,1,2,0:T(8,128)(2,1)} %copy.12) | copy-start | bytes 786436
  9.6 7.0 %collective-permute-start.7 = (bf16[4,288,128]{2,1,0:T(8,128)(2,1)S(1)}, bf16[4,288,128]{2,1,0:T(8,128)(2,1)S(1)}, u32[]{:S(2)}, u32[]{:S(2)}) collective-permute-start(bf16[4,288,128]{2,1,0:T(8,128)(2,1)S(1)} %constant_dynamic-update-slice_fusion.refs_0_), channel_id=1, source_target_pairs={{2,0},{3,1},{4,2},{5,3},{6,4},{7,5},{10,8},{11,9},{12,10},{13,11},... | collective-permute-start | bytes 884744 | tf_op jit(solution)/shard_map/ppermute | solution.py:302
  11.8 8.7 %collective-permute-start.3 = (bf16[4,288,128]{2,1,0:T(8,128)(2,1)S(1)}, bf16[4,288,128]{2,1,0:T(8,128)(2,1)S(1)}, u32[]{:S(2)}, u32[]{:S(2)}) collective-permute-start(bf16[4,288,128]{2,1,0:T(8,128)(2,1)S(1)} %constant_dynamic-update-slice_fusion.refs_0_), channel_id=1, source_target_pairs={{0,2},{1,3},{2,4},{3,5},{4,6},{5,7},{8,10},{9,11},{10,12},{11,13},... | collective-permute-start | bytes 884744 | tf_op jit(solution)/shard_map/ppermute | solution.py:302
  16.6 25.2 %copy-start.3 = (bf16[4,288,128]{2,1,0:T(8,128)(2,1)}, bf16[4,288,128]{2,1,0:T(8,128)(2,1)S(1)}, u32[]{:S(2)}) copy-start(bf16[4,288,128]{2,1,0:T(8,128)(2,1)S(1)} %collective-permute-done.7.refs_4_) | copy-start | bytes 884740
  16.6 7.9 %collective-permute-start.8 = (bf16[4,288,128]{2,1,0:T(8,128)(2,1)S(1)}, bf16[4,288,128]{2,1,0:T(8,128)(2,1)S(1)}, u32[]{:S(2)}, u32[]{:S(2)}) collective-permute-start(bf16[4,288,128]{2,1,0:T(8,128)(2,1)S(1)} %collective-permute-done.7.refs_4_), channel_id=1, source_target_pairs={{2,0},{3,1},{4,2},{5,3},{10,8},{11,9},{12,10},{13,11},{18,16},{19,... | collective-permute-start | bytes 884744 | tf_op jit(solution)/shard_map/ppermute | solution.py:302
  20.5 21.4 %copy-start.4 = (bf16[4,288,128]{2,1,0:T(8,128)(2,1)}, bf16[4,288,128]{2,1,0:T(8,128)(2,1)S(1)}, u32[]{:S(2)}) copy-start(bf16[4,288,128]{2,1,0:T(8,128)(2,1)S(1)} %collective-permute-done.3.refs_2_) | copy-start | bytes 884740
  20.5 7.8 %collective-permute-start.4 = (bf16[4,288,128]{2,1,0:T(8,128)(2,1)S(1)}, bf16[4,288,128]{2,1,0:T(8,128)(2,1)S(1)}, u32[]{:S(2)}, u32[]{:S(2)}) collective-permute-start(bf16[4,288,128]{2,1,0:T(8,128)(2,1)S(1)} %collective-permute-done.3.refs_2_), channel_id=1, source_target_pairs={{2,4},{3,5},{4,6},{5,7},{10,12},{11,13},{12,14},{13,15},{18,20},{1... | collective-permute-start | bytes 884744 | tf_op jit(solution)/shard_map/ppermute | solution.py:302
  21.8 11.4 %collective-permute-start.11 = (bf16[4,288,128]{2,1,0:T(8,128)(2,1)S(1)}, bf16[4,288,128]{2,1,0:T(8,128)(2,1)S(1)}, u32[]{:S(2)}, u32[]{:S(2)}) collective-permute-start(bf16[4,288,128]{2,1,0:T(8,128)(2,1)S(1)} %constant_dynamic-update-slice_fusion.refs_0_), channel_id=1, source_target_pairs={{0,1},{1,0},{2,3},{3,2},{4,5},{5,4},{6,7},{7,6},{8,9},{9,8},{10,11... | collective-permute-start | bytes 884744 | tf_op jit(solution)/shard_map/ppermute | solution.py:305
  24.5 8.8 %collective-permute-start.13 = (bf16[4,288,128]{2,1,0:T(8,128)(2,1)S(1)}, bf16[4,288,128]{2,1,0:T(8,128)(2,1)S(1)}, u32[]{:S(2)}, u32[]{:S(2)}) collective-permute-start(bf16[4,288,128]{2,1,0:T(8,128)(2,1)S(1)} %collective-permute-done.7.refs_4_), channel_id=1, source_target_pairs={{0,1},{1,0},{2,3},{3,2},{4,5},{5,4},{6,7},{7,6},{8,9},{9,8},{10,11... | collective-permute-start | bytes 884744 | tf_op jit(solution)/shard_map/ppermute | solution.py:305
  24.6 17.3 %copy-start.5 = (bf16[4,288,128]{2,1,0:T(8,128)(2,1)}, bf16[4,288,128]{2,1,0:T(8,128)(2,1)S(1)}, u32[]{:S(2)}) copy-start(bf16[4,288,128]{2,1,0:T(8,128)(2,1)S(1)} %collective-permute-done.8.refs_8_) | copy-start | bytes 884740
  24.6 9.4 %collective-permute-start.9 = (bf16[4,288,128]{2,1,0:T(8,128)(2,1)S(1)}, bf16[4,288,128]{2,1,0:T(8,128)(2,1)S(1)}, u32[]{:S(2)}, u32[]{:S(2)}) collective-permute-start(bf16[4,288,128]{2,1,0:T(8,128)(2,1)S(1)} %collective-permute-done.8.refs_8_), channel_id=1, source_target_pairs={{2,0},{3,1},{10,8},{11,9},{18,16},{19,17},{26,24},{27,25}} | collective-permute-start | bytes 884744 | tf_op jit(solution)/shard_map/ppermute | solution.py:302
  28.3 13.6 %copy-start.6 = (bf16[4,288,128]{2,1,0:T(8,128)(2,1)}, bf16[4,288,128]{2,1,0:T(8,128)(2,1)S(1)}, u32[]{:S(2)}) copy-start(bf16[4,288,128]{2,1,0:T(8,128)(2,1)S(1)} %collective-permute-done.4.refs_6_) | copy-start | bytes 884740
  28.3 7.5 %collective-permute-start.5 = (bf16[4,288,128]{2,1,0:T(8,128)(2,1)S(1)}, bf16[4,288,128]{2,1,0:T(8,128)(2,1)S(1)}, u32[]{:S(2)}, u32[]{:S(2)}) collective-permute-start(bf16[4,288,128]{2,1,0:T(8,128)(2,1)S(1)} %collective-permute-done.4.refs_6_), channel_id=1, source_target_pairs={{4,6},{5,7},{12,14},{13,15},{20,22},{21,23},{28,30},{29,31}} | collective-permute-start | bytes 884744 | tf_op jit(solution)/shard_map/ppermute | solution.py:302
  29.6 10.8 %collective-permute-start.12 = (bf16[4,288,128]{2,1,0:T(8,128)(2,1)S(1)}, bf16[4,288,128]{2,1,0:T(8,128)(2,1)S(1)}, u32[]{:S(2)}, u32[]{:S(2)}) collective-permute-start(bf16[4,288,128]{2,1,0:T(8,128)(2,1)S(1)} %collective-permute-done.3.refs_2_), channel_id=1, source_target_pairs={{0,1},{1,0},{2,3},{3,2},{4,5},{5,4},{6,7},{7,6},{8,9},{9,8},{10,11... | collective-permute-start | bytes 884744 | tf_op jit(solution)/shard_map/ppermute | solution.py:305
  33.1 8.7 %copy-start.7 = (bf16[4,288,128]{2,1,0:T(8,128)(2,1)}, bf16[4,288,128]{2,1,0:T(8,128)(2,1)S(1)}, u32[]{:S(2)}) copy-start(bf16[4,288,128]{2,1,0:T(8,128)(2,1)S(1)} %collective-permute-done.11.refs_1_) | copy-start | bytes 884740
  33.1 7.3 %collective-permute-start.15 = (bf16[4,288,128]{2,1,0:T(8,128)(2,1)S(1)}, bf16[4,288,128]{2,1,0:T(8,128)(2,1)S(1)}, u32[]{:S(2)}, u32[]{:S(2)}) collective-permute-start(bf16[4,288,128]{2,1,0:T(8,128)(2,1)S(1)} %collective-permute-done.8.refs_8_), channel_id=1, source_target_pairs={{0,1},{1,0},{2,3},{3,2},{4,5},{5,4},{6,7},{7,6},{8,9},{9,8},{10,11... | collective-permute-start | bytes 884744 | tf_op jit(solution)/shard_map/ppermute | solution.py:305
  33.2 0.7 %copy-start.8 = (bf16[4,288,128]{2,1,0:T(8,128)(2,1)}, bf16[4,288,128]{2,1,0:T(8,128)(2,1)S(1)}, u32[]{:S(2)}) copy-start(bf16[4,288,128]{2,1,0:T(8,128)(2,1)S(1)} %collective-permute-done.13.refs_5_) | copy-start | bytes 884740
  33.2 8.6 %collective-permute-start.14 = (bf16[4,288,128]{2,1,0:T(8,128)(2,1)S(1)}, bf16[4,288,128]{2,1,0:T(8,128)(2,1)}, u32[]{:S(2)}, u32[]{:S(2)}) collective-permute-start(bf16[4,288,128]{2,1,0:T(8,128)(2,1)S(1)} %collective-permute-done.4.refs_6_), channel_id=1, source_target_pairs={{0,1},{1,0},{2,3},{3,2},{4,5},{5,4},{6,7},{7,6},{8,9},{9,8},{10,11... | collective-permute-start | bytes 884744 | tf_op jit(solution)/shard_map/ppermute | solution.py:305
  34.0 12.8 %collective-permute-start.10 = (bf16[4,288,128]{2,1,0:T(8,128)(2,1)S(1)}, bf16[4,288,128]{2,1,0:T(8,128)(2,1)S(1)}, u32[]{:S(2)}, u32[]{:S(2)}) collective-permute-start(bf16[4,288,128]{2,1,0:T(8,128)(2,1)S(1)} %collective-permute-done.9.refs_2_), channel_id=1, source_target_pairs={{0,1},{1,0},{2,3},{3,2},{4,5},{5,4},{6,7},{7,6},{8,9},{9,8},{10,11... | collective-permute-start | bytes 884744 | tf_op jit(solution)/shard_map/ppermute | solution.py:305
  35.7 11.1 %collective-permute-start.6 = (bf16[4,288,128]{2,1,0:T(8,128)(2,1)S(1)}, bf16[4,288,128]{2,1,0:T(8,128)(2,1)S(1)}, u32[]{:S(2)}, u32[]{:S(2)}) collective-permute-start(bf16[4,288,128]{2,1,0:T(8,128)(2,1)S(1)} %collective-permute-done.5.refs_0_), channel_id=1, source_target_pairs={{0,1},{1,0},{2,3},{3,2},{4,5},{5,4},{6,7},{7,6},{8,9},{9,8},{10,11... | collective-permute-start | bytes 884744 | tf_op jit(solution)/shard_map/ppermute | solution.py:305
  40.4 0.7 %copy-start.9 = (bf16[4,288,128]{2,1,0:T(8,128)(2,1)}, bf16[4,288,128]{2,1,0:T(8,128)(2,1)S(1)}, u32[]{:S(2)}) copy-start(bf16[4,288,128]{2,1,0:T(8,128)(2,1)S(1)} %collective-permute-done.12.refs_3_) | copy-start | bytes 884740
  41.1 0.7 %copy-start.10 = (bf16[4,288,128]{2,1,0:T(8,128)(2,1)}, bf16[4,288,128]{2,1,0:T(8,128)(2,1)S(1)}, u32[]{:S(2)}) copy-start(bf16[4,288,128]{2,1,0:T(8,128)(2,1)S(1)} %collective-permute-done.15.refs_9_) | copy-start | bytes 884740

commit v3 on v2

--- a/solution.py
+++ b/solution.py
@@ -57,8 +57,14 @@
         me, place = lax.axis_index("span"), lax.axis_index("model")
         z, first = place // CORES, (place % CORES) == 0
 
+        def offset_of(s):
+            offset = slots[s][0]
+            if isinstance(offset, int):
+                return offset
+            return jnp.where(z + offset[0] >= 0, offset[0], offset[1])
+
         def block(s, k):
-            return (me ^ k) * zs + z + slots[s][0]
+            return (me ^ k) * zs + z + offset_of(s)
 
         def key_copies(s):
             for k in range(spans):
@@ -119,12 +125,14 @@
                 copy.start()
 
         base = 0
-        for s, (offset, chunks) in enumerate(slots):
-            there = (z + offset >= 0) & (z + offset < zs)
+        for s, (_, chunks) in enumerate(slots):
+            at = z + offset_of(s)
+            there = (at >= 0) & (at < zs)
             pl.when(there)(lambda s=s, base=base: work(s, base))
             base += 2 * len(chunks)
-        for s, (offset, _) in enumerate(slots):
-            there = (z + offset >= 0) & (z + offset < zs)
+        for s in range(len(slots)):
+            at = z + offset_of(s)
+            there = (at >= 0) & (at < zs)
 
             @pl.when(there)
             def _(s=s):
@@ -293,23 +301,31 @@
         return expand_spans(order, chunks, keys_t, value_up, count, rot, width, spans)
     own = [jnp.concatenate(parts[j * size : (j + 1) * size], axis=0) for j in range(CHUNKS)]
 
-    def hop(x, way, far):
-        pairs = []
-        for z in range(zs):
-            if 0 <= z + way < zs and 0 <= z - way * far < zs:
-                for c in range(CORES):
-                    pairs.append((z * CORES + c, (z + way) * CORES + c))
-        return lax.ppermute(x, "model", pairs)
+    def steps(way, far):
+        return [
+            (z * CORES + c, (z + way) * CORES + c)
+            for z in range(zs)
+            if 0 <= z + way < zs and 0 <= z - way * far < zs
+            for c in range(CORES)
+        ]
 
     def paired(x):
         return (x, lax.ppermute(x, "model", swap))
 
-    slots = [[(0, [paired(x) for x in own])]]
-    moving = {1: own, -1: own}
+    z = lax.axis_index("model") // CORES
+    up = down = merged = own[0]
+    slots = [[(0, [paired(own[0])])]]
     for d in range(1, zs):
-        for way in (1, -1):
-            moving[way] = [hop(x, way, d - 1) for x in moving[way]]
-        slots.append([(-way * d, [paired(x) for x in moving[way]]) for way in (1, -1)])
+        if merged is not up:
+            merged = lax.ppermute(merged, "model", steps(1, d - 1) + steps(-1, d - 1))
+        else:
+            up = lax.ppermute(up, "model", steps(1, d - 1))
+            down = lax.ppermute(down, "model", steps(-1, d - 1))
+            merged = jnp.where(z >= d, up, down) if 2 * d >= zs else up
+        if 2 * d >= zs:
+            slots.append([((-d, d), [paired(merged)])])
+        else:
+            slots.append([(-d, [paired(up)]), (d, [paired(down)])])
     groups = [sum(slots[:-1], []), slots[-1]]
     outs = ()
     for n, group in enumerate(groups):

time: 48.7 us -> 48.6 us (level)
  the two profiles are of different devices: /device:TPU:27 before, /device:TPU:31 now
where the time goes in v3:
time: 48.6 us; the launch traced here: 48.2 us
  starting transfers between devices  18.2 us (37%)
  waiting for transfers between devices  15.2 us (31%)
  Pallas kernels  7.88 us (16%)
  local copies, waits for them, and re-layouts  6.03 us (12%)
  between operations  0.86 us (2%)
    ppermute x2, waiting for transfers between devices, decode(): up = lax.ppermute(up, 'model', steps(1, d - 1))  9.65 us
    ppermute x5, starting transfers between devices, paired(): return (x, lax.ppermute(x, 'model', swap))  8.82 us
    pallas_call x2, Pallas kernels, expand(): pl.pallas_call(body, in_specs=[VMEM] * (len(arrays) + 2) + [HBM] * len(be...  6.07 us
    unnamed x24, local copies, waits for them, and re-layouts  4.2 us
    ppermute x2, waiting for transfers between devices, decode(): down = lax.ppermute(down, 'model', steps(-1, d - 1))  3.51 us
    ppermute x2, starting transfers between devices, decode(): down = lax.ppermute(down, 'model', steps(-1, d - 1))  2.76 us
    ppermute x3, starting transfers between devices, decode(): lax.ppermute(packed[k], 'span', [(i, i ^ k) for i in range(spans)])  2.65 us
    ppermute x2, starting transfers between devices, decode(): up = lax.ppermute(up, 'model', steps(1, d - 1))  2.57 us
  transfers between devices with their start and end apart: 13, of which 4 were waited for; matrix products, arithmetic and copies ran while one was open for 9% of the time, Pallas kernels for 10%

profile of v3, /device:TPU:31, one launch (start us, length us, event | category | flops | bytes accessed | tf_op | source)
XLA Modules:
  0.0 48.2 jit_solution(9049472250128158779)
XLA Ops:
  0.6 1.8 %pack.1 = (bf16[1,288,128]{2,1,0:T(8,128)(2,1)}, bf16[1,288,128]{2,1,0:T(8,128)(2,1)}, bf16[1,288,128]{2,1,0:T(8,128)(2,1)}, bf16[1,288,128]{2,1,0:T(8,128)(2,1)}) custom-call(bf16[4,64,512]{2,1,0:T(8,128)(2,1)} %rows_ref.1, bf16[4,64,64]{2,1,0:T(8,128)(2,1)} %rotary_ref.1, f32[1,512]{1,0:T(1,128)} %bitcast.15), custom_call_target="tpu_custom_call" | custom-call | tf_op jit(solution)/shard_map/pack/pallas_call | solution.py:36
  2.4 0.3 collective-permute-start
  2.7 0.2 collective-permute-start.1
  2.9 2.2 %collective-permute-start.2 = (bf16[1,288,128]{2,1,0:T(8,128)(2,1)}, bf16[1,288,128]{2,1,0:T(8,128)(2,1)S(1)}, u32[]{:S(2)}, u32[]{:S(2)}) collective-permute-start(bf16[1,288,128]{2,1,0:T(8,128)(2,1)} %get-tuple-element.18), channel_id=1, source_target_pairs={{0,24},{8,16},{16,8},{24,0},{1,25},{9,17},{17,9},{25,1},{2,26},{10... | collective-permute-start | bytes 221192 | tf_op jit(solution)/shard_map/ppermute | solution.py:288
  5.1 1.8 %copy.9 = bf16[2,128,512]{2,1,0:T(8,128)(2,1)} copy(bf16[2,128,512]{1,0,2:T(2,128)(2,1)} %bitcast.13) | data formatting | bytes 524288 | tf_op jit(solution)/shard_map/transpose | solution.py:282
  6.9 1.7 %copy.12 = bf16[64,8,2,128]{3,1,2,0:T(8,128)(2,1)} copy(bf16[64,8,2,128]{3,2,1,0:T(2,128)(2,1)} %bitcast.14) | data formatting | bytes 524288
  8.6 0.9 %constant_dynamic-update-slice_fusion.3 = bf16[4,288,128]{2,1,0:T(8,128)(2,1)S(1)} fusion(bf16[1,288,128]{2,1,0:T(8,128)(2,1)} %get-tuple-element.15), kind=kLoop, calls=%fused_computation.5 | loop fusion | bytes 147456
  9.5 0.0 collective-permute-done.1
  9.6 2.1 %collective-permute-start.5 = (bf16[4,288,128]{2,1,0:T(8,128)(2,1)S(1)}, bf16[4,288,128]{2,1,0:T(8,128)(2,1)S(1)}, u32[]{:S(2)}, u32[]{:S(2)}) collective-permute-start(bf16[4,288,128]{2,1,0:T(8,128)(2,1)S(1)} %constant_dynamic-update-slice_fusion.refs_0_), channel_id=1, source_target_pairs={{2,0},{3,1},{4,2},{5,3},{6,4},{7,5},{10,8},{11,9},{12,10},{13,11},... | collective-permute-start | bytes 884744 | tf_op jit(solution)/shard_map/ppermute | solution.py:323
  11.7 1.3 %collective-permute-start.3 = (bf16[4,288,128]{2,1,0:T(8,128)(2,1)S(1)}, bf16[4,288,128]{2,1,0:T(8,128)(2,1)S(1)}, u32[]{:S(2)}, u32[]{:S(2)}) collective-permute-start(bf16[4,288,128]{2,1,0:T(8,128)(2,1)S(1)} %constant_dynamic-update-slice_fusion.refs_0_), channel_id=1, source_target_pairs={{0,2},{1,3},{2,4},{3,5},{4,6},{5,7},{8,10},{9,11},{10,12},{11,13},... | collective-permute-start | bytes 884744 | tf_op jit(solution)/shard_map/ppermute | solution.py:322
  13.0 3.5 %collective-permute-done.5.refs_4_ = bf16[4,288,128]{2,1,0:T(8,128)(2,1)S(1)} collective-permute-done((bf16[4,288,128]{2,1,0:T(8,128)(2,1)S(1)}, bf16[4,288,128]{2,1,0:T(8,128)(2,1)S(1)}, u32[]{:S(2)}, u32[]{:S(2)}) %collective-permute-start.5) | collective-permute-done | bytes 294944 | tf_op jit(solution)/shard_map/ppermute | solution.py:323
  16.5 0.7 %collective-permute-start.6 = (bf16[4,288,128]{2,1,0:T(8,128)(2,1)S(1)}, bf16[4,288,128]{2,1,0:T(8,128)(2,1)S(1)}, u32[]{:S(2)}, u32[]{:S(2)}) collective-permute-start(bf16[4,288,128]{2,1,0:T(8,128)(2,1)S(1)} %collective-permute-done.5.refs_4_), channel_id=1, source_target_pairs={{2,0},{3,1},{4,2},{5,3},{10,8},{11,9},{12,10},{13,11},{18,16},{19,... | collective-permute-start | bytes 884744 | tf_op jit(solution)/shard_map/ppermute | solution.py:323
  17.2 3.2 %collective-permute-done.3.refs_2_ = bf16[4,288,128]{2,1,0:T(8,128)(2,1)S(1)} collective-permute-done((bf16[4,288,128]{2,1,0:T(8,128)(2,1)S(1)}, bf16[4,288,128]{2,1,0:T(8,128)(2,1)S(1)}, u32[]{:S(2)}, u32[]{:S(2)}) %collective-permute-start.3) | collective-permute-done | bytes 294944 | tf_op jit(solution)/shard_map/ppermute | solution.py:322
  20.4 1.3 %collective-permute-start.4 = (bf16[4,288,128]{2,1,0:T(8,128)(2,1)S(1)}, bf16[4,288,128]{2,1,0:T(8,128)(2,1)S(1)}, u32[]{:S(2)}, u32[]{:S(2)}) collective-permute-start(bf16[4,288,128]{2,1,0:T(8,128)(2,1)S(1)} %collective-permute-done.3.refs_2_), channel_id=1, source_target_pairs={{2,4},{3,5},{4,6},{5,7},{10,12},{11,13},{12,14},{13,15},{18,20},{1... | collective-permute-start | bytes 884744 | tf_op jit(solution)/shard_map/ppermute | solution.py:322
  21.7 0.0 collective-permute-done.6
  21.7 6.5 %collective-permute-done.4 = bf16[4,288,128]{2,1,0:T(8,128)(2,1)S(1)} collective-permute-done((bf16[4,288,128]{2,1,0:T(8,128)(2,1)S(1)}, bf16[4,288,128]{2,1,0:T(8,128)(2,1)S(1)}, u32[]{:S(2)}, u32[]{:S(2)}) %collective-permute-start.4) | collective-permute-done | bytes 294944 | tf_op jit(solution)/shard_map/ppermute | solution.py:322
  28.2 1.4 %collective-permute-start.7 = (bf16[4,288,128]{2,1,0:T(8,128)(2,1)S(1)}, bf16[4,288,128]{2,1,0:T(8,128)(2,1)S(1)}, u32[]{:S(2)}, u32[]{:S(2)}) collective-permute-start(bf16[4,288,128]{2,1,0:T(8,128)(2,1)S(1)} %broadcast_select_fusion.refs_6_), channel_id=1, source_target_pairs={{4,6},{5,7},{2,0},{3,1},{12,14},{13,15},{10,8},{11,9},{20,22},{21,... | collective-permute-start | bytes 884744 | tf_op jit(solution)/shard_map/ppermute | solution.py:320
  29.6 3.6 %collective-permute-start.9 = (bf16[4,288,128]{2,1,0:T(8,128)(2,1)S(1)}, bf16[4,288,128]{2,1,0:T(8,128)(2,1)S(1)}, u32[]{:S(2)}, u32[]{:S(2)}) collective-permute-start(bf16[4,288,128]{2,1,0:T(8,128)(2,1)S(1)} %constant_dynamic-update-slice_fusion.refs_0_), channel_id=1, source_target_pairs={{0,1},{1,0},{2,3},{3,2},{4,5},{5,4},{6,7},{7,6},{8,9},{9,8},{10,11... | collective-permute-start | bytes 884744 | tf_op jit(solution)/shard_map/ppermute | solution.py:313
  33.2 0.1 collective-permute-start.11
  33.3 0.4 collective-permute-start.10
  33.7 0.1 collective-permute-start.12
  33.8 2.0 %collective-permute-done.7.refs_0_ = bf16[4,288,128]{2,1,0:T(8,128)(2,1)S(1)} collective-permute-done((bf16[4,288,128]{2,1,0:T(8,128)(2,1)S(1)}, bf16[4,288,128]{2,1,0:T(8,128)(2,1)S(1)}, u32[]{:S(2)}, u32[]{:S(2)}) %collective-permute-start.7) | collective-permute-done | bytes 294944 | tf_op jit(solution)/shard_map/ppermute | solution.py:320
  35.8 4.7 %collective-permute-start.8 = (bf16[4,288,128]{2,1,0:T(8,128)(2,1)S(1)}, bf16[4,288,128]{2,1,0:T(8,128)(2,1)S(1)}, u32[]{:S(2)}, u32[]{:S(2)}) collective-permute-start(bf16[4,288,128]{2,1,0:T(8,128)(2,1)S(1)} %collective-permute-done.7.refs_0_), channel_id=1, source_target_pairs={{0,1},{1,0},{2,3},{3,2},{4,5},{5,4},{6,7},{7,6},{8,9},{9,8},{10,11... | collective-permute-start | bytes 884744 | tf_op jit(solution)/shard_map/ppermute | solution.py:313
  40.5 0.0 collective-permute-done.9.refs_1_
  40.5 0.0 collective-permute-done.10.refs_3_
  40.5 0.0 collective-permute-done.12.refs_7_
  40.6 0.6 %copy-done.6 = bf16[4,288,128]{2,1,0:T(8,128)(2,1)} copy-done((bf16[4,288,128]{2,1,0:T(8,128)(2,1)}, bf16[4,288,128]{2,1,0:T(8,128)(2,1)S(1)}, u32[]{:S(2)}) %copy-start.6) | copy-done | bytes 294936
  41.2 0.1 copy-done.7
  41.3 0.1 copy-done.8
  41.4 0.7 %copy-done.9 = bf16[4,288,128]{2,1,0:T(8,128)(2,1)} copy-done((bf16[4,288,128]{2,1,0:T(8,128)(2,1)}, bf16[4,288,128]{2,1,0:T(8,128)(2,1)S(1)}, u32[]{:S(2)}) %copy-start.9) | copy-done | bytes 294936
  42.1 4.6 %shard_map.68 = (bf16[1,2,192,2048]{3,2,1,0:T(8,128)(2,1)}, bf16[4096,128]{1,0:T(8,128)(2,1)}) custom-call(bf16[4,288,128]{2,1,0:T(8,128)(2,1)} %copy-done.3, bf16[4,288,128]{2,1,0:T(8,128)(2,1)} %copy-done.6, bf16[4,288,128]{2,1,0:T(8,128)(2,1)} %copy-done.5, bf16[4,288,128]{2,1,0:T(8,128)(2,1)} %copy-done.8, bf16[4,288,128]{2,1,0:T(8,128)(2,1)} %copy-done.4, ...), custom_call_target="tpu_custom_call" | custom-call | tf_op jit(solution)/shard_map/pallas_call | solution.py:146
  46.8 1.4 %shard_map.69 = (bf16[1,2,192,2048]{3,2,1,0:T(8,128)(2,1)}, bf16[4096,128]{1,0:T(8,128)(2,1)}) custom-call(bf16[4,288,128]{2,1,0:T(8,128)(2,1)S(1)} %collective-permute-done.7.refs_0_, bf16[4,288,128]{2,1,0:T(8,128)(2,1)S(1)} %collective-permute-done.8.refs_1_, bf16[256,512]{1,0:T(8,128)(2,1)S(1)} %bitcast.9, ...), custom_call_target="tpu_custom_call", output_to_operand_aliasing={{0}: (4, {}), {1}: (5, {})} | custom-call | tf_op jit(solution)/shard_map/pallas_call | solution.py:146
  (24 shorter events, 0.1 us)
Async XLA Ops:
  2.4 7.1 %collective-permute-start = (bf16[1,288,128]{2,1,0:T(8,128)(2,1)}, bf16[1,288,128]{2,1,0:T(8,128)(2,1)S(1)}, u32[]{:S(2)}, u32[]{:S(2)}) collective-permute-start(bf16[1,288,128]{2,1,0:T(8,128)(2,1)} %get-tuple-element.16), channel_id=1, source_target_pairs={{0,8},{8,0},{16,24},{24,16},{1,9},{9,1},{17,25},{25,17},{2,10},{10... | collective-permute-start | bytes 221192 | tf_op jit(solution)/shard_map/ppermute | solution.py:288
  2.7 6.8 %collective-permute-start.1 = (bf16[1,288,128]{2,1,0:T(8,128)(2,1)}, bf16[1,288,128]{2,1,0:T(8,128)(2,1)S(1)}, u32[]{:S(2)}, u32[]{:S(2)}) collective-permute-start(bf16[1,288,128]{2,1,0:T(8,128)(2,1)} %get-tuple-element.17), channel_id=1, source_target_pairs={{0,16},{8,24},{16,0},{24,8},{1,17},{9,25},{17,1},{25,9},{2,18},{10... | collective-permute-start | bytes 221192 | tf_op jit(solution)/shard_map/ppermute | solution.py:288
  2.9 6.6 %collective-permute-start.2 = (bf16[1,288,128]{2,1,0:T(8,128)(2,1)}, bf16[1,288,128]{2,1,0:T(8,128)(2,1)S(1)}, u32[]{:S(2)}, u32[]{:S(2)}) collective-permute-start(bf16[1,288,128]{2,1,0:T(8,128)(2,1)} %get-tuple-element.18), channel_id=1, source_target_pairs={{0,24},{8,16},{16,8},{24,0},{1,25},{9,17},{17,9},{25,1},{2,26},{10... | collective-permute-start | bytes 221192 | tf_op jit(solution)/shard_map/ppermute | solution.py:288
  9.6 30.9 %copy-start.3 = (bf16[4,288,128]{2,1,0:T(8,128)(2,1)}, bf16[4,288,128]{2,1,0:T(8,128)(2,1)S(1)}, u32[]{:S(2)}) copy-start(bf16[4,288,128]{2,1,0:T(8,128)(2,1)S(1)} %constant_dynamic-update-slice_fusion.refs_0_) | copy-start | bytes 884740
  9.6 6.9 %collective-permute-start.5 = (bf16[4,288,128]{2,1,0:T(8,128)(2,1)S(1)}, bf16[4,288,128]{2,1,0:T(8,128)(2,1)S(1)}, u32[]{:S(2)}, u32[]{:S(2)}) collective-permute-start(bf16[4,288,128]{2,1,0:T(8,128)(2,1)S(1)} %constant_dynamic-update-slice_fusion.refs_0_), channel_id=1, source_target_pairs={{2,0},{3,1},{4,2},{5,3},{6,4},{7,5},{10,8},{11,9},{12,10},{13,11},... | collective-permute-start | bytes 884744 | tf_op jit(solution)/shard_map/ppermute | solution.py:323
  11.7 8.7 %collective-permute-start.3 = (bf16[4,288,128]{2,1,0:T(8,128)(2,1)S(1)}, bf16[4,288,128]{2,1,0:T(8,128)(2,1)S(1)}, u32[]{:S(2)}, u32[]{:S(2)}) collective-permute-start(bf16[4,288,128]{2,1,0:T(8,128)(2,1)S(1)} %constant_dynamic-update-slice_fusion.refs_0_), channel_id=1, source_target_pairs={{0,2},{1,3},{2,4},{3,5},{4,6},{5,7},{8,10},{9,11},{10,12},{11,13},... | collective-permute-start | bytes 884744 | tf_op jit(solution)/shard_map/ppermute | solution.py:322
  16.5 24.0 %copy-start.4 = (bf16[4,288,128]{2,1,0:T(8,128)(2,1)}, bf16[4,288,128]{2,1,0:T(8,128)(2,1)S(1)}, u32[]{:S(2)}) copy-start(bf16[4,288,128]{2,1,0:T(8,128)(2,1)S(1)} %collective-permute-done.5.refs_4_) | copy-start | bytes 884740
  16.5 5.2 %collective-permute-start.6 = (bf16[4,288,128]{2,1,0:T(8,128)(2,1)S(1)}, bf16[4,288,128]{2,1,0:T(8,128)(2,1)S(1)}, u32[]{:S(2)}, u32[]{:S(2)}) collective-permute-start(bf16[4,288,128]{2,1,0:T(8,128)(2,1)S(1)} %collective-permute-done.5.refs_4_), channel_id=1, source_target_pairs={{2,0},{3,1},{4,2},{5,3},{10,8},{11,9},{12,10},{13,11},{18,16},{19,... | collective-permute-start | bytes 884744 | tf_op jit(solution)/shard_map/ppermute | solution.py:323
  20.4 20.2 %copy-start.5 = (bf16[4,288,128]{2,1,0:T(8,128)(2,1)}, bf16[4,288,128]{2,1,0:T(8,128)(2,1)S(1)}, u32[]{:S(2)}) copy-start(bf16[4,288,128]{2,1,0:T(8,128)(2,1)S(1)} %collective-permute-done.3.refs_2_) | copy-start | bytes 884740
  20.4 7.8 %collective-permute-start.4 = (bf16[4,288,128]{2,1,0:T(8,128)(2,1)S(1)}, bf16[4,288,128]{2,1,0:T(8,128)(2,1)S(1)}, u32[]{:S(2)}, u32[]{:S(2)}) collective-permute-start(bf16[4,288,128]{2,1,0:T(8,128)(2,1)S(1)} %collective-permute-done.3.refs_2_), channel_id=1, source_target_pairs={{2,4},{3,5},{4,6},{5,7},{10,12},{11,13},{12,14},{13,15},{18,20},{1... | collective-permute-start | bytes 884744 | tf_op jit(solution)/shard_map/ppermute | solution.py:322
  28.2 12.4 %copy-start.2 = (bf16[4,288,128]{2,1,0:T(8,128)(2,1)}, bf16[4,288,128]{2,1,0:T(8,128)(2,1)S(1)}, u32[]{:S(2)}) copy-start(bf16[4,288,128]{2,1,0:T(8,128)(2,1)S(1)} %broadcast_select_fusion.refs_6_) | copy-start | bytes 884740
  28.2 18.6 %copy-start = (bf16[2,128,512]{2,1,0:T(8,128)(2,1)S(1)}, bf16[2,128,512]{2,1,0:T(8,128)(2,1)}, u32[]{:S(2)}) copy-start(bf16[2,128,512]{2,1,0:T(8,128)(2,1)} %copy.9) | copy-start | bytes 786436
  28.2 18.6 %copy-start.1 = (bf16[64,8,2,128]{3,1,2,0:T(8,128)(2,1)S(1)}, bf16[64,8,2,128]{3,1,2,0:T(8,128)(2,1)}, u32[]{:S(2)}) copy-start(bf16[64,8,2,128]{3,1,2,0:T(8,128)(2,1)} %copy.12) | copy-start | bytes 786436
  28.2 7.6 %collective-permute-start.7 = (bf16[4,288,128]{2,1,0:T(8,128)(2,1)S(1)}, bf16[4,288,128]{2,1,0:T(8,128)(2,1)S(1)}, u32[]{:S(2)}, u32[]{:S(2)}) collective-permute-start(bf16[4,288,128]{2,1,0:T(8,128)(2,1)S(1)} %broadcast_select_fusion.refs_6_), channel_id=1, source_target_pairs={{4,6},{5,7},{2,0},{3,1},{12,14},{13,15},{10,8},{11,9},{20,22},{21,... | collective-permute-start | bytes 884744 | tf_op jit(solution)/shard_map/ppermute | solution.py:320
  29.6 10.8 %collective-permute-start.9 = (bf16[4,288,128]{2,1,0:T(8,128)(2,1)S(1)}, bf16[4,288,128]{2,1,0:T(8,128)(2,1)S(1)}, u32[]{:S(2)}, u32[]{:S(2)}) collective-permute-start(bf16[4,288,128]{2,1,0:T(8,128)(2,1)S(1)} %constant_dynamic-update-slice_fusion.refs_0_), channel_id=1, source_target_pairs={{0,1},{1,0},{2,3},{3,2},{4,5},{5,4},{6,7},{7,6},{8,9},{9,8},{10,11... | collective-permute-start | bytes 884744 | tf_op jit(solution)/shard_map/ppermute | solution.py:313
  33.2 7.3 %collective-permute-start.11 = (bf16[4,288,128]{2,1,0:T(8,128)(2,1)S(1)}, bf16[4,288,128]{2,1,0:T(8,128)(2,1)S(1)}, u32[]{:S(2)}, u32[]{:S(2)}) collective-permute-start(bf16[4,288,128]{2,1,0:T(8,128)(2,1)S(1)} %collective-permute-done.5.refs_4_), channel_id=1, source_target_pairs={{0,1},{1,0},{2,3},{3,2},{4,5},{5,4},{6,7},{7,6},{8,9},{9,8},{10,11... | collective-permute-start | bytes 884744 | tf_op jit(solution)/shard_map/ppermute | solution.py:313
  33.3 7.2 %collective-permute-start.10 = (bf16[4,288,128]{2,1,0:T(8,128)(2,1)S(1)}, bf16[4,288,128]{2,1,0:T(8,128)(2,1)S(1)}, u32[]{:S(2)}, u32[]{:S(2)}) collective-permute-start(bf16[4,288,128]{2,1,0:T(8,128)(2,1)S(1)} %collective-permute-done.3.refs_2_), channel_id=1, source_target_pairs={{0,1},{1,0},{2,3},{3,2},{4,5},{5,4},{6,7},{7,6},{8,9},{9,8},{10,11... | collective-permute-start | bytes 884744 | tf_op jit(solution)/shard_map/ppermute | solution.py:313
  33.7 6.8 %collective-permute-start.12 = (bf16[4,288,128]{2,1,0:T(8,128)(2,1)S(1)}, bf16[4,288,128]{2,1,0:T(8,128)(2,1)S(1)}, u32[]{:S(2)}, u32[]{:S(2)}) collective-permute-start(bf16[4,288,128]{2,1,0:T(8,128)(2,1)S(1)} %broadcast_select_fusion.refs_6_), channel_id=1, source_target_pairs={{0,1},{1,0},{2,3},{3,2},{4,5},{5,4},{6,7},{7,6},{8,9},{9,8},{10,11... | collective-permute-start | bytes 884744 | tf_op jit(solution)/shard_map/ppermute | solution.py:313
  35.8 11.0 %collective-permute-start.8 = (bf16[4,288,128]{2,1,0:T(8,128)(2,1)S(1)}, bf16[4,288,128]{2,1,0:T(8,128)(2,1)S(1)}, u32[]{:S(2)}, u32[]{:S(2)}) collective-permute-start(bf16[4,288,128]{2,1,0:T(8,128)(2,1)S(1)} %collective-permute-done.7.refs_0_), channel_id=1, source_target_pairs={{0,1},{1,0},{2,3},{3,2},{4,5},{5,4},{6,7},{7,6},{8,9},{9,8},{10,11... | collective-permute-start | bytes 884744 | tf_op jit(solution)/shard_map/ppermute | solution.py:313
  40.5 0.7 %copy-start.6 = (bf16[4,288,128]{2,1,0:T(8,128)(2,1)}, bf16[4,288,128]{2,1,0:T(8,128)(2,1)S(1)}, u32[]{:S(2)}) copy-start(bf16[4,288,128]{2,1,0:T(8,128)(2,1)S(1)} %collective-permute-done.9.refs_1_) | copy-start | bytes 884740
  40.5 0.8 %copy-start.7 = (bf16[4,288,128]{2,1,0:T(8,128)(2,1)}, bf16[4,288,128]{2,1,0:T(8,128)(2,1)S(1)}, u32[]{:S(2)}) copy-start(bf16[4,288,128]{2,1,0:T(8,128)(2,1)S(1)} %collective-permute-done.11.refs_5_) | copy-start | bytes 884740
  40.5 0.9 %copy-start.8 = (bf16[4,288,128]{2,1,0:T(8,128)(2,1)}, bf16[4,288,128]{2,1,0:T(8,128)(2,1)S(1)}, u32[]{:S(2)}) copy-start(bf16[4,288,128]{2,1,0:T(8,128)(2,1)S(1)} %collective-permute-done.10.refs_3_) | copy-start | bytes 884740
  41.4 0.7 %copy-start.9 = (bf16[4,288,128]{2,1,0:T(8,128)(2,1)}, bf16[4,288,128]{2,1,0:T(8,128)(2,1)S(1)}, u32[]{:S(2)}) copy-start(bf16[4,288,128]{2,1,0:T(8,128)(2,1)S(1)} %collective-permute-done.12.refs_7_) | copy-start | bytes 884740
